TPU v7x, 128 devices: a whole 4x4x4 slice. The times are simulated.
128 devices in a mesh: south: 4 (over x), east: 8 (over y, core), down: 4 (over z).
Axes of the slice: x: 4, y: 4, z: 4, core: 2. Of those that a mesh axis runs over, the one named last changes fastest.
Arguments:
- field_now: float32 [32, 128, 512, 128], P('south', 'east', 'down'), may hold values from 0.2 to 1.8
- earlier: float32 [32, 128, 512, 128], P('south', 'east', 'down'), may hold values from 0.2 to 1.8
- speed_square: float32 [32, 128, 512, 128], P('south', 'east', 'down'), may hold values from 0.05 to 0.3
Outputs:
- running_total: float32 [32, 128, 512, 128], P('south', 'east', 'down')
- field_now_end: float32 [32, 128, 512, 128], P('south', 'east', 'down')
All inputs are finite; a program needn't handle non-finite values.
Results may differ from a plain program's by a relative error of at most 0.00002.
Values sent between devices are 32-bit elements; how exact they have to be, the bound alone decides.
A program may use at most 320 MiB of HBM per device.

v0:
```python
import jax
import jax.numpy as jnp
from jax import lax
from jax.sharding import PartitionSpec as P

STEPS = 4


def with_halo(array, sides, width):
    edges = {}
    for axis, dim in sides:
        count, length = (lax.axis_size(axis), array.shape[dim])
        up = [(i, (i + 1) % count) for i in range(count - 1)]
        last = lax.slice_in_dim(array, length - width, length, axis=dim)
        initial = lax.slice_in_dim(array, 0, width, axis=dim)
        edges[dim] = (
            lax.ppermute(last, axis, up),
            lax.ppermute(initial, axis, [(b, a) for a, b in up]),
        )
    done = []
    for _, dim in sides:
        low, high = edges[dim]
        around = [(width, width) if d in done else (0, 0) for d in range(array.ndim)]
        array = jnp.concatenate([jnp.pad(low, around), array, jnp.pad(high, around)], axis=dim)
        done.append(dim)
    return array


def prefix(part, axis, combine, identity):
    place = lax.axis_index(axis)
    gathered = lax.all_gather(part, axis)
    state = jnp.zeros_like(part) + jnp.asarray(identity, part.dtype)

    def one(turn, state):
        return combine(state, lax.dynamic_index_in_dim(gathered, turn, 0, False))

    return lax.fori_loop(0, place, one, state)


def strip_edges(values, dims):
    for dim in dims:
        values = lax.slice_in_dim(values, 1, values.shape[dim] - 1, axis=dim)
    return values


def neighbour(values, dim, start, dims):
    others = [other for other in dims if other != dim]
    values = strip_edges(values, others)
    return lax.slice_in_dim(values, start, start + values.shape[dim] - 2, axis=dim)


def one_step(padded, before, speed_square):
    middle = strip_edges(padded, (0, 1, 2))
    lower = [neighbour(padded, dim, 0, (0, 1, 2)) for dim in (0, 1, 2)]
    upper = [neighbour(padded, dim, 2, (0, 1, 2)) for dim in (0, 1, 2)]
    spread = lower[0] + upper[0] + lower[1] + upper[1] + lower[2] + upper[2] - 6.0 * middle
    return 2.0 * middle - before + speed_square * spread


def shards(field_now, earlier, speed_square):
    for step in range(STEPS):
        padded = with_halo(field_now, (("south", 0), ("east", 1), ("down", 2)), 1)
        later = one_step(padded, earlier, speed_square)
        earlier, field_now = (field_now, later)
    here = jnp.cumsum(field_now, axis=0)
    total = lax.slice_in_dim(here, here.shape[0] - 1, here.shape[0], axis=0)

    def add_pair(earlier_total, later_total):
        return earlier_total + later_total

    below = prefix(total, "south", add_pair, jnp.zeros_like(total))
    running_total = (here + below) / (field_now.shape[0] * lax.axis_size("south"))
    return (running_total, field_now)


def solution(mesh):
    placed = (
        P("south", "east", "down", None),
        P("south", "east", "down", None),
        P("south", "east", "down", None),
    )
    return jax.shard_map(
        shards,
        mesh=mesh,
        in_specs=placed,
        out_specs=(P("south", "east", "down", None), P("south", "east", "down", None)),
        check_vma=False,
    )
```

profile of v0, /device:TPU:103, one launch (start us, length us, event | category | flops | bytes accessed | tf_op | source)
XLA Modules:
  0.0 322.0 jit_solution(2014024687277370611)
XLA Ops:
  7.2 1.8 fusion.51
  10.6 4.1 %collective-permute-start.1 = (f32[1,16,128,128]{3,2,1,0:T(8,128)S(1)}, f32[1,16,128,128]{3,2,1,0:T(8,128)S(1)}, u32[]{:S(2)}, u32[]{:S(2)}) collective-permute-start(f32[1,16,128,128]{3,2,1,0:T(8,128)S(1)} %get-tuple-element.64), channel_id=1, source_target_pairs={{32,0},{64,32},{96,64},{33,1},{65,33},{97,65},{34,2},{66,34},{98,6... | collective-permute-start | bytes 3145736 | tf_op jit(solution)/shard_map/ppermute | solution.py:18
  16.0 4.3 %collective-permute-start.2 = (f32[8,1,128,128]{3,2,1,0:T(8,128)S(1)}, f32[8,1,128,128]{3,2,1,0:T(8,128)S(1)}, u32[]{:S(2)}, u32[]{:S(2)}) collective-permute-start(f32[8,1,128,128]{3,2,1,0:T(8,128)S(1)} %get-tuple-element.62), channel_id=1, source_target_pairs={{0,4},{4,8},{8,12},{12,16},{16,20},{20,24},{24,28},{1,5},{5,9},{9,... | collective-permute-start | bytes 1572872 | tf_op jit(solution)/shard_map/ppermute | solution.py:17
  20.3 1.9 collective-permute-start.3
  26.4 2.4 collective-permute-start.5
  32.0 3.3 %collective-permute-done = f32[1,16,128,128]{3,2,1,0:T(8,128)S(1)} collective-permute-done((f32[1,16,128,128]{3,2,1,0:T(8,128)S(1)}, f32[1,16,128,128]{3,2,1,0:T(8,128)S(1)}, u32[]{:S(2)}, u32[]{:S(2)}) %collective-permute-start) | collective-permute-done | bytes 1048608 | tf_op jit(solution)/shard_map/ppermute | solution.py:17
  36.4 4.8 %constant_dynamic-update-slice_fusion.1 = f32[10,16,128,128]{3,2,1,0:T(8,128)} fusion(f32[10,16,128,128]{3,2,1,0:T(8,128)} %constant_dynamic-update-slice_fusion.2, f32[8,16,128,128]{3,2,1,0:T(8,128)S(1)} %copy-done), kind=kLoop, calls=%fused_computation.109 | loop fusion | bytes 16777216
  43.2 28.2 %fusion.34 = f32[8,16,128,128]{3,2,1,0:T(8,128)} fusion(f32[8,16,128,128]{3,2,1,0:T(8,128)S(1)} %bitcast.10, f32[8,16,1,128]{3,2,1,0:T(1,128)S(1)} %collective-permute-done.5, f32[10,1,128,128]{3,2,1,0:T(8,128)} %pad.51, f32[10,16,128,128]{3,2,1,0:T(8,128)} %constant_dynamic-update-slice_fusion, f32[10,1,128,128]{3,2,1,0:T(8,128)} %pad.50, ...), kind=kLoop, calls=%fused_computation.90 | loop fusion | flops 56623104 | bytes 47579136 | tf_op jit(solution)/shard_map/add | solution.py:57
  74.3 4.1 %collective-permute-start.7 = (f32[1,16,128,128]{3,2,1,0:T(8,128)S(1)}, f32[1,16,128,128]{3,2,1,0:T(8,128)S(1)}, u32[]{:S(2)}, u32[]{:S(2)}) collective-permute-start(f32[1,16,128,128]{3,2,1,0:T(8,128)S(1)} %get-tuple-element.57), channel_id=1, source_target_pairs={{32,0},{64,32},{96,64},{33,1},{65,33},{97,65},{34,2},{66,34},{98,6... | collective-permute-start | bytes 3145736 | tf_op jit(solution)/shard_map/ppermute | solution.py:18
  79.7 5.2 %collective-permute-start.8 = (f32[8,1,128,128]{3,2,1,0:T(8,128)S(1)}, f32[8,1,128,128]{3,2,1,0:T(8,128)S(1)}, u32[]{:S(2)}, u32[]{:S(2)}) collective-permute-start(f32[8,1,128,128]{3,2,1,0:T(8,128)S(1)} %get-tuple-element.58), channel_id=1, source_target_pairs={{0,4},{4,8},{8,12},{12,16},{16,20},{20,24},{24,28},{1,5},{5,9},{9,... | collective-permute-start | bytes 1572872 | tf_op jit(solution)/shard_map/ppermute | solution.py:17
  84.9 1.9 collective-permute-start.9
  91.0 2.4 collective-permute-start.11
  93.5 2.2 collective-permute-done.9
  95.7 2.4 collective-permute-done.6
  99.0 28.2 %fusion.24 = f32[8,16,128,128]{3,2,1,0:T(8,128)} fusion(f32[8,16,128,128]{3,2,1,0:T(8,128)} %param.7, f32[8,16,1,128]{3,2,1,0:T(1,128)S(1)} %collective-permute-done.11, f32[10,1,128,128]{3,2,1,0:T(8,128)S(1)} %pad.55, f32[10,1,128,128]{3,2,1,0:T(8,128)S(1)} %pad.54, f32[1,16,128,128]{3,2,1,0:T(8,128)S(1)} %collective-permute-done.7, ...), kind=kLoop, calls=%fused_computation.62 | loop fusion | flops 73400320 | bytes 37093376 | tf_op jit(solution)/shard_map/add | solution.py:57
  130.2 4.8 %collective-permute-start.13 = (f32[1,16,128,128]{3,2,1,0:T(8,128)S(1)}, f32[1,16,128,128]{3,2,1,0:T(8,128)S(1)}, u32[]{:S(2)}, u32[]{:S(2)}) collective-permute-start(f32[1,16,128,128]{3,2,1,0:T(8,128)S(1)} %get-tuple-element.51), channel_id=1, source_target_pairs={{32,0},{64,32},{96,64},{33,1},{65,33},{97,65},{34,2},{66,34},{98,6... | collective-permute-start | bytes 3145736 | tf_op jit(solution)/shard_map/ppermute | solution.py:18
  136.3 6.0 %collective-permute-start.14 = (f32[8,1,128,128]{3,2,1,0:T(8,128)S(1)}, f32[8,1,128,128]{3,2,1,0:T(8,128)S(1)}, u32[]{:S(2)}, u32[]{:S(2)}) collective-permute-start(f32[8,1,128,128]{3,2,1,0:T(8,128)S(1)} %get-tuple-element.52), channel_id=1, source_target_pairs={{0,4},{4,8},{8,12},{12,16},{16,20},{20,24},{24,28},{1,5},{5,9},{9,... | collective-permute-start | bytes 1572872 | tf_op jit(solution)/shard_map/ppermute | solution.py:17
  142.4 1.9 collective-permute-start.15
  148.5 2.6 collective-permute-start.17
  151.1 2.0 collective-permute-done.15
  154.8 28.2 %fusion.14 = f32[8,16,128,128]{3,2,1,0:T(8,128)} fusion(f32[8,16,128,128]{3,2,1,0:T(8,128)} %param.7, f32[8,16,1,128]{3,2,1,0:T(1,128)S(1)} %collective-permute-done.17, f32[10,1,128,128]{3,2,1,0:T(8,128)S(1)} %pad.59, f32[10,1,128,128]{3,2,1,0:T(8,128)S(1)} %pad.58, f32[1,16,128,128]{3,2,1,0:T(8,128)S(1)} %collective-permute-done.13, ...), kind=kLoop, calls=%fused_computation.34 | loop fusion | flops 73400320 | bytes 37093376 | tf_op jit(solution)/shard_map/add | solution.py:57
  186.0 4.8 %collective-permute-start.19 = (f32[1,16,128,128]{3,2,1,0:T(8,128)S(1)}, f32[1,16,128,128]{3,2,1,0:T(8,128)S(1)}, u32[]{:S(2)}, u32[]{:S(2)}) collective-permute-start(f32[1,16,128,128]{3,2,1,0:T(8,128)S(1)} %get-tuple-element.45), channel_id=1, source_target_pairs={{32,0},{64,32},{96,64},{33,1},{65,33},{97,65},{34,2},{66,34},{98,6... | collective-permute-start | bytes 3145736 | tf_op jit(solution)/shard_map/ppermute | solution.py:18
  192.1 6.9 %collective-permute-start.20 = (f32[8,1,128,128]{3,2,1,0:T(8,128)S(1)}, f32[8,1,128,128]{3,2,1,0:T(8,128)S(1)}, u32[]{:S(2)}, u32[]{:S(2)}) collective-permute-start(f32[8,1,128,128]{3,2,1,0:T(8,128)S(1)} %get-tuple-element.46), channel_id=1, source_target_pairs={{0,4},{4,8},{8,12},{12,16},{16,20},{20,24},{24,28},{1,5},{5,9},{9,... | collective-permute-start | bytes 1572872 | tf_op jit(solution)/shard_map/ppermute | solution.py:17
  199.0 1.9 collective-permute-start.21
  205.1 2.4 collective-permute-start.23
  207.6 2.2 collective-permute-done.21
  209.9 28.2 %fusion.4 = f32[8,16,128,128]{3,2,1,0:T(8,128)} fusion(f32[8,16,128,128]{3,2,1,0:T(8,128)} %param.7, f32[8,16,1,128]{3,2,1,0:T(1,128)S(1)} %collective-permute-done.23, f32[10,1,128,128]{3,2,1,0:T(8,128)S(1)} %pad.63, f32[10,1,128,128]{3,2,1,0:T(8,128)S(1)} %pad.62, f32[1,16,128,128]{3,2,1,0:T(8,128)S(1)} %collective-permute-done.19, ...), kind=kLoop, calls=%fused_computation.6 | loop fusion | flops 73400320 | bytes 37093376 | tf_op jit(solution)/shard_map/add | solution.py:57
  238.1 8.5 %fusion.52 = f32[8,16,128,128]{3,2,1,0:T(8,128)} fusion(f32[8,16,128,128]{3,2,1,0:T(8,128)} %fusion.4), kind=kOutput, calls=%fused_computation.123 | output fusion | flops 14680064 | bytes 16777216 | tf_op jit(solution)/shard_map/jit(cumsum)/reduce_window_sum | solution.py:65
  246.6 2.3 slice.370
  248.9 53.0 %all-gather.3.cloned.1.call-done = f32[4,16,128,128]{3,2,1,0:T(8,128)} async-done(((f32[1,16,128,128]{3,2,1,0:T(8,128)}), f32[4,16,128,128]{3,2,1,0:T(8,128)}) %all-gather.3.cloned.1.call-update) | async-done | bytes 4194320 | tf_op jit(solution)/shard_map/all_gather | solution.py:31
  302.0 4.6 %while.10 = (s32[]{:T(128)}, f32[1,16,128,128]{3,2,1,0:T(8,128)S(1)}, s32[]{:T(128)}, f32[4,1,16,128,128]{4,3,2,1,0:T(8,128)}, s32[]{:T(128)}, /*index=5*/s32[]{:T(128)}, s32[]{:T(128)}) while((s32[]{:T(128)}, f32[1,16,128,128]{3,2,1,0:T(8,128)S(1)}, s32[]{:T(128)}, f32[4,1,16,128,128]{4,3,2,1,0:T(8,128)}, s32[]{:T(128)}, ...), condition=%wide.region_2.3_spmd, body=%wide.region_1.2_spmd.sunk | while | flops 262149 | bytes 3145843 | solution.py:37
  306.6 8.6 %add_multiply_fusion = f32[8,16,128,128]{3,2,1,0:T(8,128)} fusion(f32[8,16,128,128]{3,2,1,0:T(8,128)} %fusion.52, f32[16,128,128]{2,1,0:T(8,128)S(1)} %bitcast.11), kind=kLoop, calls=%fused_computation.107 | loop fusion | flops 4194304 | bytes 17825792 | tf_op jit(solution)/shard_map/div | solution.py:72
  (63 shorter events, 45.9 us)
Async XLA Ops:
  7.2 294.7 %all-gather.3.cloned.1.call-start = ((), (), s32[]{:S(2)}) async-start(), calls=%async_computation | async-start | bytes 5242880 | tf_op jit(solution)/shard_map/all_gather | solution.py:31
  7.2 29.1 %copy-start = (f32[8,16,128,128]{3,2,1,0:T(8,128)S(1)}, f32[8,16,128,128]{3,2,1,0:T(8,128)}, u32[]{:S(2)}) copy-start(f32[8,16,128,128]{3,2,1,0:T(8,128)} %param.5) | copy-start | bytes 25165828
  9.1 26.2 %collective-permute-start = (f32[1,16,128,128]{3,2,1,0:T(8,128)S(1)}, f32[1,16,128,128]{3,2,1,0:T(8,128)S(1)}, u32[]{:S(2)}, u32[]{:S(2)}) collective-permute-start(f32[1,16,128,128]{3,2,1,0:T(8,128)S(1)} %get-tuple-element.65), channel_id=1, source_target_pairs={{0,32},{32,64},{64,96},{1,33},{33,65},{65,97},{2,34},{34,66},{66,9... | collective-permute-start | bytes 3145736 | tf_op jit(solution)/shard_map/ppermute | solution.py:17
  10.6 30.5 %collective-permute-start.1 = (f32[1,16,128,128]{3,2,1,0:T(8,128)S(1)}, f32[1,16,128,128]{3,2,1,0:T(8,128)S(1)}, u32[]{:S(2)}, u32[]{:S(2)}) collective-permute-start(f32[1,16,128,128]{3,2,1,0:T(8,128)S(1)} %get-tuple-element.64), channel_id=1, source_target_pairs={{32,0},{64,32},{96,64},{33,1},{65,33},{97,65},{34,2},{66,34},{98,6... | collective-permute-start | bytes 3145736 | tf_op jit(solution)/shard_map/ppermute | solution.py:18
  16.0 10.4 %collective-permute-start.2 = (f32[8,1,128,128]{3,2,1,0:T(8,128)S(1)}, f32[8,1,128,128]{3,2,1,0:T(8,128)S(1)}, u32[]{:S(2)}, u32[]{:S(2)}) collective-permute-start(f32[8,1,128,128]{3,2,1,0:T(8,128)S(1)} %get-tuple-element.62), channel_id=1, source_target_pairs={{0,4},{4,8},{8,12},{12,16},{16,20},{20,24},{24,28},{1,5},{5,9},{9,... | collective-permute-start | bytes 1572872 | tf_op jit(solution)/shard_map/ppermute | solution.py:17
  20.3 10.8 %collective-permute-start.3 = (f32[8,1,128,128]{3,2,1,0:T(8,128)S(1)}, f32[8,1,128,128]{3,2,1,0:T(8,128)S(1)}, u32[]{:S(2)}, u32[]{:S(2)}) collective-permute-start(f32[8,1,128,128]{3,2,1,0:T(8,128)S(1)} %get-tuple-element.63), channel_id=1, source_target_pairs={{4,0},{8,4},{12,8},{16,12},{20,16},{24,20},{28,24},{5,1},{9,5},{13... | collective-permute-start | bytes 1572872 | tf_op jit(solution)/shard_map/ppermute | solution.py:18
  23.5 19.6 %collective-permute-start.4 = (f32[8,16,1,128]{3,2,1,0:T(1,128)S(1)}, f32[8,16,1,128]{3,2,1,0:T(1,128)S(1)}, u32[]{:S(2)}, u32[]{:S(2)}) collective-permute-start(f32[8,16,1,128]{3,2,1,0:T(1,128)S(1)} %get-tuple-element.60), channel_id=1, source_target_pairs={{0,1},{1,2},{2,3},{4,5},{5,6},{6,7},{8,9},{9,10},{10,11},{12,13},{... | collective-permute-start | bytes 196616 | tf_op jit(solution)/shard_map/ppermute | solution.py:17
  26.4 16.7 %collective-permute-start.5 = (f32[8,16,1,128]{3,2,1,0:T(1,128)S(1)}, f32[8,16,1,128]{3,2,1,0:T(1,128)S(1)}, u32[]{:S(2)}, u32[]{:S(2)}) collective-permute-start(f32[8,16,1,128]{3,2,1,0:T(1,128)S(1)} %get-tuple-element.61), channel_id=1, source_target_pairs={{1,0},{2,1},{3,2},{5,4},{6,5},{7,6},{9,8},{10,9},{11,10},{13,12},{... | collective-permute-start | bytes 196616 | tf_op jit(solution)/shard_map/ppermute | solution.py:18
  35.3 7.9 %slice-start = ((s8[8388608]{0:T(1024)(128)(4,1)}), s8[4194304]{0:T(1024)(128)(4,1)S(1)}, s32[]{:S(2)}) async-start(s8[8388608]{0:T(1024)(128)(4,1)} %bitcast.9), calls=%async_computation.1 | async-start | bytes 8388608
  36.3 6.8 %slice-start.1 = ((s8[8388608]{0:T(1024)(128)(4,1)}), s8[4194304]{0:T(1024)(128)(4,1)S(1)}, s32[]{:S(2)}) async-start(s8[8388608]{0:T(1024)(128)(4,1)} %bitcast.9), calls=%async_computation.2 | async-start | bytes 8388608
  41.1 1.0 copy-start.1
  73.0 25.1 %collective-permute-start.6 = (f32[1,16,128,128]{3,2,1,0:T(8,128)S(1)}, f32[1,16,128,128]{3,2,1,0:T(8,128)S(1)}, u32[]{:S(2)}, u32[]{:S(2)}) collective-permute-start(f32[1,16,128,128]{3,2,1,0:T(8,128)S(1)} %get-tuple-element.56), channel_id=1, source_target_pairs={{0,32},{32,64},{64,96},{1,33},{33,65},{65,97},{2,34},{34,66},{66,9... | collective-permute-start | bytes 3145736 | tf_op jit(solution)/shard_map/ppermute | solution.py:17
  74.3 24.7 %collective-permute-start.7 = (f32[1,16,128,128]{3,2,1,0:T(8,128)S(1)}, f32[1,16,128,128]{3,2,1,0:T(8,128)S(1)}, u32[]{:S(2)}, u32[]{:S(2)}) collective-permute-start(f32[1,16,128,128]{3,2,1,0:T(8,128)S(1)} %get-tuple-element.57), channel_id=1, source_target_pairs={{32,0},{64,32},{96,64},{33,1},{65,33},{97,65},{34,2},{66,34},{98,6... | collective-permute-start | bytes 3145736 | tf_op jit(solution)/shard_map/ppermute | solution.py:18
  79.7 11.3 %collective-permute-start.8 = (f32[8,1,128,128]{3,2,1,0:T(8,128)S(1)}, f32[8,1,128,128]{3,2,1,0:T(8,128)S(1)}, u32[]{:S(2)}, u32[]{:S(2)}) collective-permute-start(f32[8,1,128,128]{3,2,1,0:T(8,128)S(1)} %get-tuple-element.58), channel_id=1, source_target_pairs={{0,4},{4,8},{8,12},{12,16},{16,20},{20,24},{24,28},{1,5},{5,9},{9,... | collective-permute-start | bytes 1572872 | tf_op jit(solution)/shard_map/ppermute | solution.py:17
  84.9 10.8 %collective-permute-start.9 = (f32[8,1,128,128]{3,2,1,0:T(8,128)S(1)}, f32[8,1,128,128]{3,2,1,0:T(8,128)S(1)}, u32[]{:S(2)}, u32[]{:S(2)}) collective-permute-start(f32[8,1,128,128]{3,2,1,0:T(8,128)S(1)} %get-tuple-element.59), channel_id=1, source_target_pairs={{4,0},{8,4},{12,8},{16,12},{20,16},{24,20},{28,24},{5,1},{9,5},{13... | collective-permute-start | bytes 1572872 | tf_op jit(solution)/shard_map/ppermute | solution.py:18
  88.1 7.6 %collective-permute-start.10 = (f32[8,16,1,128]{3,2,1,0:T(1,128)S(1)}, f32[8,16,1,128]{3,2,1,0:T(1,128)S(1)}, u32[]{:S(2)}, u32[]{:S(2)}) collective-permute-start(f32[8,16,1,128]{3,2,1,0:T(1,128)S(1)} %get-tuple-element.54), channel_id=1, source_target_pairs={{0,1},{1,2},{2,3},{4,5},{5,6},{6,7},{8,9},{9,10},{10,11},{12,13},{... | collective-permute-start | bytes 196616 | tf_op jit(solution)/shard_map/ppermute | solution.py:17
  91.0 4.8 %collective-permute-start.11 = (f32[8,16,1,128]{3,2,1,0:T(1,128)S(1)}, f32[8,16,1,128]{3,2,1,0:T(1,128)S(1)}, u32[]{:S(2)}, u32[]{:S(2)}) collective-permute-start(f32[8,16,1,128]{3,2,1,0:T(1,128)S(1)} %get-tuple-element.55), channel_id=1, source_target_pairs={{1,0},{2,1},{3,2},{5,4},{6,5},{7,6},{9,8},{10,9},{11,10},{13,12},{... | collective-permute-start | bytes 196616 | tf_op jit(solution)/shard_map/ppermute | solution.py:18
  128.9 25.0 %collective-permute-start.12 = (f32[1,16,128,128]{3,2,1,0:T(8,128)S(1)}, f32[1,16,128,128]{3,2,1,0:T(8,128)S(1)}, u32[]{:S(2)}, u32[]{:S(2)}) collective-permute-start(f32[1,16,128,128]{3,2,1,0:T(8,128)S(1)} %get-tuple-element.50), channel_id=1, source_target_pairs={{0,32},{32,64},{64,96},{1,33},{33,65},{65,97},{2,34},{34,66},{66,9... | collective-permute-start | bytes 3145736 | tf_op jit(solution)/shard_map/ppermute | solution.py:17
  130.2 24.6 %collective-permute-start.13 = (f32[1,16,128,128]{3,2,1,0:T(8,128)S(1)}, f32[1,16,128,128]{3,2,1,0:T(8,128)S(1)}, u32[]{:S(2)}, u32[]{:S(2)}) collective-permute-start(f32[1,16,128,128]{3,2,1,0:T(8,128)S(1)} %get-tuple-element.51), channel_id=1, source_target_pairs={{32,0},{64,32},{96,64},{33,1},{65,33},{97,65},{34,2},{66,34},{98,6... | collective-permute-start | bytes 3145736 | tf_op jit(solution)/shard_map/ppermute | solution.py:18
  136.3 12.1 %collective-permute-start.14 = (f32[8,1,128,128]{3,2,1,0:T(8,128)S(1)}, f32[8,1,128,128]{3,2,1,0:T(8,128)S(1)}, u32[]{:S(2)}, u32[]{:S(2)}) collective-permute-start(f32[8,1,128,128]{3,2,1,0:T(8,128)S(1)} %get-tuple-element.52), channel_id=1, source_target_pairs={{0,4},{4,8},{8,12},{12,16},{16,20},{20,24},{24,28},{1,5},{5,9},{9,... | collective-permute-start | bytes 1572872 | tf_op jit(solution)/shard_map/ppermute | solution.py:17
  142.4 10.8 %collective-permute-start.15 = (f32[8,1,128,128]{3,2,1,0:T(8,128)S(1)}, f32[8,1,128,128]{3,2,1,0:T(8,128)S(1)}, u32[]{:S(2)}, u32[]{:S(2)}) collective-permute-start(f32[8,1,128,128]{3,2,1,0:T(8,128)S(1)} %get-tuple-element.53), channel_id=1, source_target_pairs={{4,0},{8,4},{12,8},{16,12},{20,16},{24,20},{28,24},{5,1},{9,5},{13... | collective-permute-start | bytes 1572872 | tf_op jit(solution)/shard_map/ppermute | solution.py:18
  145.6 7.6 %collective-permute-start.16 = (f32[8,16,1,128]{3,2,1,0:T(1,128)S(1)}, f32[8,16,1,128]{3,2,1,0:T(1,128)S(1)}, u32[]{:S(2)}, u32[]{:S(2)}) collective-permute-start(f32[8,16,1,128]{3,2,1,0:T(1,128)S(1)} %get-tuple-element.48), channel_id=1, source_target_pairs={{0,1},{1,2},{2,3},{4,5},{5,6},{6,7},{8,9},{9,10},{10,11},{12,13},{... | collective-permute-start | bytes 196616 | tf_op jit(solution)/shard_map/ppermute | solution.py:17
  148.5 4.8 %collective-permute-start.17 = (f32[8,16,1,128]{3,2,1,0:T(1,128)S(1)}, f32[8,16,1,128]{3,2,1,0:T(1,128)S(1)}, u32[]{:S(2)}, u32[]{:S(2)}) collective-permute-start(f32[8,16,1,128]{3,2,1,0:T(1,128)S(1)} %get-tuple-element.49), channel_id=1, source_target_pairs={{1,0},{2,1},{3,2},{5,4},{6,5},{7,6},{9,8},{10,9},{11,10},{13,12},{... | collective-permute-start | bytes 196616 | tf_op jit(solution)/shard_map/ppermute | solution.py:18
  184.7 25.2 %collective-permute-start.18 = (f32[1,16,128,128]{3,2,1,0:T(8,128)S(1)}, f32[1,16,128,128]{3,2,1,0:T(8,128)S(1)}, u32[]{:S(2)}, u32[]{:S(2)}) collective-permute-start(f32[1,16,128,128]{3,2,1,0:T(8,128)S(1)} %get-tuple-element.44), channel_id=1, source_target_pairs={{0,32},{32,64},{64,96},{1,33},{33,65},{65,97},{2,34},{34,66},{66,9... | collective-permute-start | bytes 3145736 | tf_op jit(solution)/shard_map/ppermute | solution.py:17
  186.0 23.9 %collective-permute-start.19 = (f32[1,16,128,128]{3,2,1,0:T(8,128)S(1)}, f32[1,16,128,128]{3,2,1,0:T(8,128)S(1)}, u32[]{:S(2)}, u32[]{:S(2)}) collective-permute-start(f32[1,16,128,128]{3,2,1,0:T(8,128)S(1)} %get-tuple-element.45), channel_id=1, source_target_pairs={{32,0},{64,32},{96,64},{33,1},{65,33},{97,65},{34,2},{66,34},{98,6... | collective-permute-start | bytes 3145736 | tf_op jit(solution)/shard_map/ppermute | solution.py:18
  192.1 13.0 %collective-permute-start.20 = (f32[8,1,128,128]{3,2,1,0:T(8,128)S(1)}, f32[8,1,128,128]{3,2,1,0:T(8,128)S(1)}, u32[]{:S(2)}, u32[]{:S(2)}) collective-permute-start(f32[8,1,128,128]{3,2,1,0:T(8,128)S(1)} %get-tuple-element.46), channel_id=1, source_target_pairs={{0,4},{4,8},{8,12},{12,16},{16,20},{20,24},{24,28},{1,5},{5,9},{9,... | collective-permute-start | bytes 1572872 | tf_op jit(solution)/shard_map/ppermute | solution.py:17
  199.0 10.8 %collective-permute-start.21 = (f32[8,1,128,128]{3,2,1,0:T(8,128)S(1)}, f32[8,1,128,128]{3,2,1,0:T(8,128)S(1)}, u32[]{:S(2)}, u32[]{:S(2)}) collective-permute-start(f32[8,1,128,128]{3,2,1,0:T(8,128)S(1)} %get-tuple-element.47), channel_id=1, source_target_pairs={{4,0},{8,4},{12,8},{16,12},{20,16},{24,20},{28,24},{5,1},{9,5},{13... | collective-permute-start | bytes 1572872 | tf_op jit(solution)/shard_map/ppermute | solution.py:18
  202.2 7.6 %collective-permute-start.22 = (f32[8,16,1,128]{3,2,1,0:T(1,128)S(1)}, f32[8,16,1,128]{3,2,1,0:T(1,128)S(1)}, u32[]{:S(2)}, u32[]{:S(2)}) collective-permute-start(f32[8,16,1,128]{3,2,1,0:T(1,128)S(1)} %get-tuple-element.42), channel_id=1, source_target_pairs={{0,1},{1,2},{2,3},{4,5},{5,6},{6,7},{8,9},{9,10},{10,11},{12,13},{... | collective-permute-start | bytes 196616 | tf_op jit(solution)/shard_map/ppermute | solution.py:17
  205.1 4.8 %collective-permute-start.23 = (f32[8,16,1,128]{3,2,1,0:T(1,128)S(1)}, f32[8,16,1,128]{3,2,1,0:T(1,128)S(1)}, u32[]{:S(2)}, u32[]{:S(2)}) collective-permute-start(f32[8,16,1,128]{3,2,1,0:T(1,128)S(1)} %get-tuple-element.43), channel_id=1, source_target_pairs={{1,0},{2,1},{3,2},{5,4},{6,5},{7,6},{9,8},{10,9},{11,10},{13,12},{... | collective-permute-start | bytes 196616 | tf_op jit(solution)/shard_map/ppermute | solution.py:18
Sparse Core Ops, SparseCore 0:
  249.0 52.8 all-gather.2
where the time goes:
time: 324 us; the launch traced here: 322 us
  other arithmetic  134 us (41%)
  waiting for transfers between devices  75.1 us (23%)
  starting transfers between devices  68.4 us (21%)
  local copies, waits for them, and re-layouts  29.6 us (9%)
  between operations  14.5 us (4%)
    add x4, other arithmetic, one_step(): return 2.0 * middle - before + speed_square * spread  113 us
    all_gather x1, waiting for transfers between devices, prefix(): gathered = lax.all_gather(part, axis)  53 us
    ppermute x12, starting transfers between devices, with_halo(): lax.ppermute(initial, axis, [(b, a) for a, b in up])  35.3 us
    ppermute x12, starting transfers between devices, with_halo(): lax.ppermute(last, axis, up)  33 us
    slice x11, local copies, waits for them, and re-layouts, with_halo(): last = lax.slice_in_dim(array, length - width, length, axis=dim)  15.4 us
    ppermute x12, waiting for transfers between devices, with_halo(): lax.ppermute(last, axis, up)  12.6 us
    ppermute x12, waiting for transfers between devices, with_halo(): lax.ppermute(initial, axis, [(b, a) for a, b in up])  9.58 us
    div x1, other arithmetic, shards(): (here + below) / (field_now.shape[0] * lax.axis_size('south'))  8.62 us
  transfers between devices with their start and end apart: 25, of which 14 were waited for; matrix products, arithmetic and copies ran while one was open for 6% of the time, Pallas kernels for 0%

commit v1 on v0

v1 whole, which is shorter than its diff:
```python
import functools

import jax
import jax.numpy as jnp
from jax import lax
from jax.experimental import pallas as pl
from jax.experimental.pallas import tpu as pltpu
from jax.sharding import PartitionSpec as P

STEPS = 4
ROWS = 4
AXES = ("south", "east", "down")


def steps_kernel(
    grid_j, u0, e0, s0, field, below, prev, speed, zsend, zrecv, total,
    load_sem, xsend_sem, xrecv_sem, ysend_sem, yrecv_sem, zsend_sem, zrecv_sem, tsend_sem, trecv_sem,
):
    nj, ni, nk, nm = s0.shape
    chunks = ni // ROWS
    place = {a: lax.axis_index(a) for a in AXES}
    count = {a: lax.axis_size(a) for a in AXES}
    has = {a: (place[a] > 0, place[a] < count[a] - 1) for a in AXES}
    peer = {a: (place[a] - 1, place[a] + 1) for a in AXES}

    inner = (pl.ds(1, nj), pl.ds(1, ni))
    loads = [
        pltpu.make_async_copy(u0, field.at[inner], load_sem.at[0]),
        pltpu.make_async_copy(e0, prev.at[inner], load_sem.at[1]),
        pltpu.make_async_copy(s0, speed, load_sem.at[2]),
    ]
    for load in loads:
        load.start()

    barrier = pltpu.get_barrier_semaphore()
    greeted = 0
    for a in AXES:
        for side in (0, 1):
            @pl.when(has[a][side])
            def _():
                pl.semaphore_signal(barrier, inc=1, device_id={a: peer[a][side]}, device_id_type=pl.DeviceIdType.MESH)
            greeted = greeted + has[a][side].astype(jnp.int32)
    pl.semaphore_wait(barrier, greeted)

    bufs = (field, prev)

    def remote(src, dst, send_sem, recv_sem, axis, side):
        return pltpu.make_async_remote_copy(
            src_ref=src, dst_ref=dst, send_sem=send_sem, recv_sem=recv_sem,
            device_id={axis: peer[axis][side]}, device_id_type=pl.DeviceIdType.MESH,
        )

    def x_copy(t, side, c, src=None):
        buf = bufs[t % 2]
        rows = pl.ds(1 + c * ROWS, ROWS)
        own, dst = (nj if side else 1), (0 if side else nj + 1)
        src = buf.at[own, rows] if src is None else src
        return remote(src, buf.at[dst, rows], xsend_sem.at[t, side, c], xrecv_sem.at[t, 1 - side, c], "south", side)

    def y_copy(t, side, src=None):
        buf = bufs[t % 2]
        own, dst = (ni if side else 1), (0 if side else ni + 1)
        src = buf.at[pl.ds(1, nj), own] if src is None else src
        return remote(src, buf.at[pl.ds(1, nj), dst], ysend_sem.at[t, side], yrecv_sem.at[t, 1 - side], "east", side)

    def z_copy(t, side, c):
        rows = pl.ds(c * ROWS, ROWS)
        return remote(
            zsend.at[t, side, rows], zrecv.at[t, 1 - side, rows],
            zsend_sem.at[t, side, c], zrecv_sem.at[t, 1 - side, c], "down", side,
        )

    def on(pred, action):
        @pl.when(pred)
        def _():
            action()

    for c in range(chunks):
        rows = pl.ds(c * ROWS, ROWS)
        for side in (1, 0):
            on(has["south"][side], lambda: x_copy(0, side, c, u0.at[nj - 1 if side else 0, rows]).start())
    for side in (1, 0):
        on(has["east"][side], lambda: y_copy(0, side, u0.at[:, ni - 1 if side else 0]).start())

    for buf in bufs:
        for side in (0, 1):
            @pl.when(jnp.logical_not(has["south"][side]))
            def _():
                def fill(i, _):
                    buf[(nj + 1) * side, i] = jnp.zeros((nk, nm), jnp.float32)
                    return 0
                lax.fori_loop(0, ni + 2, fill, 0)

            @pl.when(jnp.logical_not(has["east"][side]))
            def _():
                def fill(j, _):
                    buf[j, (ni + 1) * side] = jnp.zeros((nk, nm), jnp.float32)
                    return 0
                lax.fori_loop(1, nj + 1, fill, 0)
    for side in (0, 1):
        @pl.when(jnp.logical_not(has["down"][side]))
        def _():
            def fill(i, _):
                for t in range(STEPS):
                    zrecv[t, side, i] = jnp.zeros((nj, nm), jnp.float32)
                return 0
            lax.fori_loop(0, ni, fill, 0)

    loads[0].wait()

    def pack(i, _):
        for j in range(nj):
            zsend[0, 0, i, j : j + 1] = field[1 + j, 1 + i, 0:1]
            zsend[0, 1, i, j : j + 1] = field[1 + j, 1 + i, nk - 1 : nk]
        return 0

    lax.fori_loop(0, ni, pack, 0)

    def z_start(t, c):
        for side in (1, 0):
            on(has["down"][side], lambda: z_copy(t, side, c).start())

    def send_all_z(c, _):
        z_start(0, c)
        return 0

    lax.fori_loop(0, chunks, send_all_z, 0)
    loads[1].wait()
    loads[2].wait()

    def t_copy(i):
        return remote(total.at[i], below.at[i], tsend_sem.at[i], trecv_sem.at[i], "south", 1)

    first_row = lax.broadcasted_iota(jnp.int32, (8, nm), 0) == 0
    last_row = lax.broadcasted_iota(jnp.int32, (8, nm), 0) == 7

    for t in range(STEPS):
        src, dst = bufs[t % 2], bufs[(t + 1) % 2]
        last = t == STEPS - 1

        def chunk(c, _):
            for side in (0, 1):
                on(has["south"][side], lambda: x_copy(t, 1 - side, c).wait_recv())
                on(has["down"][side], lambda: z_copy(t, 1 - side, c).wait_recv())
            on(jnp.logical_and(has["east"][0], c == 0), lambda: y_copy(t, 1).wait_recv())
            on(jnp.logical_and(has["east"][1], c == chunks - 1), lambda: y_copy(t, 0).wait_recv())
            if t >= 2:
                for side in (0, 1):
                    on(has["south"][side], lambda: x_copy(t - 1, side, c).wait_send())
                on(jnp.logical_and(has["east"][0], c == 0), lambda: y_copy(t - 1, 0).wait_send())
                on(jnp.logical_and(has["east"][1], c == chunks - 1), lambda: y_copy(t - 1, 1).wait_send())

            def row(r, _):
                i = c * ROWS + r
                acc = None
                for j in range(nj):
                    mid = src[1 + j, 1 + i]
                    above = pltpu.roll(mid, 1, 0)
                    under = pltpu.roll(mid, nk - 1, 0)
                    zl = zrecv[t, 0, i, j : j + 1]
                    zh = zrecv[t, 1, i, j : j + 1]
                    above = jnp.concatenate([jnp.where(first_row, zl, above[:8]), above[8:]], axis=0)
                    under = jnp.concatenate([under[:-8], jnp.where(last_row, zh, under[-8:])], axis=0)
                    spread = src[j, 1 + i] + src[2 + j, 1 + i] + src[1 + j, i] + src[1 + j, 2 + i] + above + under - 6.0 * mid
                    new = 2.0 * mid - dst[1 + j, 1 + i] + speed[j, i] * spread
                    dst[1 + j, 1 + i] = new
                    if last:
                        acc = new if acc is None else acc + new
                    else:
                        zsend[t + 1, 0, i, j : j + 1] = new[0:1]
                        zsend[t + 1, 1, i, j : j + 1] = new[nk - 1 : nk]
                if last:
                    total[i] = acc
                return 0

            lax.fori_loop(0, ROWS, row, 0)
            if not last:
                for side in (1, 0):
                    on(has["south"][side], lambda: x_copy(t + 1, side, c).start())
                z_start(t + 1, c)
                on(jnp.logical_and(has["east"][0], c == 0), lambda: y_copy(t + 1, 0).start())
                on(jnp.logical_and(has["east"][1], c == chunks - 1), lambda: y_copy(t + 1, 1).start())
            else:
                def send_row(r, _):
                    t_copy(c * ROWS + r).start()
                    return 0

                @pl.when(jnp.logical_not(has["south"][0]))
                def _():
                    lax.fori_loop(0, ROWS, send_row, 0)
            return 0

        lax.fori_loop(0, chunks, chunk, 0)

    @pl.when(has["south"][0])
    def _():
        def relay(i, _):
            t_copy(i).wait_recv()
            total[i] = total[i] + below[i]
            on(has["south"][1], lambda: t_copy(i).start())
            return 0

        lax.fori_loop(0, ni, relay, 0)

    @pl.when(jnp.logical_not(has["south"][0]))
    def _():
        def fill(i, _):
            below[i] = jnp.zeros((nk, nm), jnp.float32)
            return 0

        lax.fori_loop(0, ni, fill, 0)

    @pl.when(has["south"][1])
    def _():
        def sent(i, _):
            t_copy(i).wait_send()
            return 0

        lax.fori_loop(0, ni, sent, 0)

    def drain(c, _):
        for t in range(STEPS):
            for side in (0, 1):
                if t in (0, STEPS - 1):
                    on(has["south"][side], lambda: x_copy(t, side, c).wait_send())
                on(has["down"][side], lambda: z_copy(t, side, c).wait_send())
        return 0

    lax.fori_loop(0, chunks, drain, 0)
    for t in (0, STEPS - 1):
        for side in (0, 1):
            on(has["east"][side], lambda: y_copy(t, side).wait_send())


def outputs_kernel(grid_j, field, below, running, end, stage, out_sem, field_sem):
    nj, ni, nk, nm = end.shape
    rows = 2
    groups = ni // rows
    whole = pltpu.make_async_copy(field.at[pl.ds(1, nj), pl.ds(1, ni)], end, field_sem)
    whole.start()

    def out(g):
        at = pl.ds(g * rows, rows)
        return pltpu.make_async_copy(stage.at[:, at], running.at[:, at], out_sem.at[g])

    def group(g, _):
        for r in range(rows):
            i = g * rows + r
            acc = below[i]
            for j in range(nj):
                acc = acc + field[1 + j, 1 + i]
                stage[j, i] = acc * (1.0 / grid_j)
        out(g).start()
        return 0

    lax.fori_loop(0, groups, group, 0)

    def done(g, _):
        out(g).wait()
        return 0

    lax.fori_loop(0, groups, done, 0)
    whole.wait()


def shards(field_now, earlier, speed_square):
    shape = field_now.shape
    nj, ni, nk, nm = shape
    padded = (nj + 2, ni + 2, nk, nm)
    chunks = ni // ROWS
    grid_j = nj * lax.axis_size("south")
    dma = pltpu.SemaphoreType.DMA
    anyspace = pl.BlockSpec(memory_space=pltpu.HBM)
    vmem = pl.BlockSpec(memory_space=pltpu.VMEM)
    f32 = jnp.float32
    field, below = pl.pallas_call(
        functools.partial(steps_kernel, grid_j),
        out_shape=(pltpu.VMEM(padded, f32), pltpu.VMEM((ni, nk, nm), f32)),
        in_specs=[anyspace] * 3,
        out_specs=(vmem, vmem),
        scratch_shapes=[
            pltpu.VMEM(padded, f32),
            pltpu.VMEM(shape, f32),
            pltpu.VMEM((STEPS, 2, ni, nj, nm), f32),
            pltpu.VMEM((STEPS, 2, ni, nj, nm), f32),
            pltpu.VMEM((ni, nk, nm), f32),
            dma((3,)),
            dma((STEPS, 2, chunks)), dma((STEPS, 2, chunks)),
            dma((STEPS, 2)), dma((STEPS, 2)),
            dma((STEPS, 2, chunks)), dma((STEPS, 2, chunks)),
            dma((ni,)), dma((ni,)),
        ],
        compiler_params=pltpu.CompilerParams(
            collective_id=0, has_side_effects=True, vmem_limit_bytes=36 * 1024 * 1024,
        ),
        name="steps",
    )(field_now, earlier, speed_square)
    return pl.pallas_call(
        functools.partial(outputs_kernel, grid_j),
        out_shape=(jax.ShapeDtypeStruct(shape, f32), jax.ShapeDtypeStruct(shape, f32)),
        in_specs=[vmem, vmem],
        out_specs=(anyspace, anyspace),
        scratch_shapes=[pltpu.VMEM(shape, f32), dma((ni // 2,)), dma],
        compiler_params=pltpu.CompilerParams(vmem_limit_bytes=32 * 1024 * 1024),
        name="outputs",
    )(field, below)


def solution(mesh):
    placed = P(*AXES, None)
    return jax.shard_map(
        shards,
        mesh=mesh,
        in_specs=(placed, placed, placed),
        out_specs=(placed, placed),
        check_vma=False,
    )
```

time: 324 us -> 131 us (0.40)
  other arithmetic: 134 us -> 0 us
  Pallas kernels: 0 us -> 129 us
  waiting for transfers between devices: 75.1 us -> 0 us
  starting transfers between devices: 68.4 us -> 0 us
  local copies, waits for them, and re-layouts: 29.6 us -> 0 us
  between operations: 14.5 us -> 0.64 us
    pallas_call x0 -> x2, Pallas kernels: none -> 129 us  [the longest x1 123 us: shards(): pl.pallas_call(functools.partial(steps_kernel, grid_j), out_shape=(pltpu....]
    add x7 -> x0, other arithmetic: 117 us -> none  [the longest x4 113 us: one_step(): return 2.0 * middle - before + speed_square * spread]
    ppermute x24 -> x0, starting transfers between devices: 68.3 us -> none  [the longest x12 35.3 us: with_halo(): lax.ppermute(initial, axis, [(b, a) for a, b in up])]
    all_gather x1 -> x0, waiting for transfers between devices: 53 us -> none  [prefix(): gathered = lax.all_gather(part, axis)]
    ppermute x24 -> x0, waiting for transfers between devices: 22.1 us -> none  [the longest x12 12.6 us: with_halo(): lax.ppermute(last, axis, up)]
    slice x13 -> x0, local copies, waits for them, and re-layouts: 19.6 us -> none  [the longest x11 15.4 us: with_halo(): last = lax.slice_in_dim(array, length - width, length, axis=dim)]
    div x1 -> x0, other arithmetic: 8.62 us -> none  [shards(): (here + below) / (field_now.shape[0] * lax.axis_size('south'))]
    another operation x1 -> x0, other arithmetic: 8.46 us -> none  [shards(): here = jnp.cumsum(field_now, axis=0)]
  transfers between devices with their start and end apart: 25 -> 0, of which waited for: 14 -> 0; matrix products, arithmetic and copies ran while one was open for 6% -> 0% of each run, Pallas kernels for 0% -> 0%
where the time goes in v1:
time: 131 us; the launch traced here: 130 us
  Pallas kernels  129 us (98%)
    pallas_call x1, Pallas kernels, shards(): pl.pallas_call(functools.partial(steps_kernel, grid_j), out_shape=(pltpu....  123 us
    pallas_call x1, Pallas kernels, shards(): pl.pallas_call(functools.partial(outputs_kernel, grid_j), out_shape=(jax....  6.02 us

profile of v1, /device:TPU:103, one launch (start us, length us, event | category | flops | bytes accessed | tf_op | source)
XLA Modules:
  0.0 129.6 jit_solution(1529674408674999904)
XLA Ops:
  0.6 122.9 %steps.1 = (f32[10,18,128,128]{3,2,1,0:T(8,128)S(1)}, f32[16,128,128]{2,1,0:T(8,128)S(1)}) custom-call(f32[8,16,128,128]{3,2,1,0:T(8,128)} %u0.1, f32[8,16,128,128]{3,2,1,0:T(8,128)} %e0.1, f32[8,16,128,128]{3,2,1,0:T(8,128)} %s0.1), custom_call_target="tpu_custom_call" | custom-call | tf_op jit(solution)/shard_map/steps/pallas_call | solution.py:276
  123.6 6.0 %outputs.1 = (f32[8,16,128,128]{3,2,1,0:T(8,128)}, f32[8,16,128,128]{3,2,1,0:T(8,128)}) custom-call(f32[10,18,128,128]{3,2,1,0:T(8,128)S(1)} %get-tuple-element.4.field, f32[16,128,128]{2,1,0:T(8,128)S(1)} %get-tuple-element.5.below), custom_call_target="tpu_custom_call" | custom-call | tf_op jit(solution)/shard_map/outputs/pallas_call | solution.py:298

commit v2 on v1

--- a/solution.py
+++ b/solution.py
@@ -10,11 +10,12 @@
 STEPS = 4
 ROWS = 4
 AXES = ("south", "east", "down")
+WAYS = {"G": (0,), "H": (1,), "A": (2,), "B": (3,)}
 
 
 def steps_kernel(
-    grid_j, u0, e0, s0, field, below, prev, speed, zsend, zrecv, total,
-    load_sem, xsend_sem, xrecv_sem, ysend_sem, yrecv_sem, zsend_sem, zrecv_sem, tsend_sem, trecv_sem,
+    grid_j, u0, e0, s0, field, below, prev, speed, zsend, zrecv, total, alow, ahigh, slow, shigh,
+    load_sem, xsend_sem, xrecv_sem, ysend_sem, yrecv_sem, zsend_sem, zrecv_sem, upsend_sem, uprecv_sem, downsend_sem, downrecv_sem,
 ):
     nj, ni, nk, nm = s0.shape
     chunks = ni // ROWS
@@ -33,8 +34,11 @@
         load.start()
 
     barrier = pltpu.get_barrier_semaphore()
-    greeted = 0
-    for a in AXES:
+    greeted = 2
+    ring = (lax.rem(place["south"] + count["south"] - 1, count["south"]), lax.rem(place["south"] + 1, count["south"]))
+    for side in (0, 1):
+        pl.semaphore_signal(barrier, inc=1, device_id={"south": ring[side]}, device_id_type=pl.DeviceIdType.MESH)
+    for a in AXES[1:]:
         for side in (0, 1):
             @pl.when(has[a][side])
             def _():
@@ -128,8 +132,41 @@
     loads[1].wait()
     loads[2].wait()
 
-    def t_copy(i):
-        return remote(total.at[i], below.at[i], tsend_sem.at[i], trecv_sem.at[i], "south", 1)
+    def up(src, dst, i):
+        return pltpu.make_async_remote_copy(
+            src_ref=src.at[i], dst_ref=dst.at[i], send_sem=upsend_sem.at[i], recv_sem=uprecv_sem.at[i],
+            device_id={"south": ring[1]}, device_id_type=pl.DeviceIdType.MESH,
+        )
+
+    def down(src, dst, i):
+        return pltpu.make_async_remote_copy(
+            src_ref=src.at[i], dst_ref=dst.at[i], send_sem=downsend_sem.at[i], recv_sem=downrecv_sem.at[i],
+            device_id={"south": ring[0]}, device_id_type=pl.DeviceIdType.MESH,
+        )
+
+    ways = {w: [c * ROWS + r for c in cs for r in range(ROWS)] for w, cs in WAYS.items()}
+    first = {
+        0: (("G", down, ahigh), ("A", up, below), ("B", up, below), ("H", up, below)),
+        1: (("G", up, alow), ("H", down, ahigh)),
+        2: (("H", up, alow), ("B", down, ahigh)),
+        3: (),
+    }
+
+    def send_totals(c):
+        for x, sends in first.items():
+            ready = []
+            latest = {"up": 0, "down": 0}
+            for w, go, target in sends:
+                key = "up" if go is up else "down"
+                latest[key] = max(latest[key], max(WAYS[w]))
+                if latest[key] == c:
+                    ready.append((w, go, target))
+            if ready:
+                @pl.when(place["south"] == x)
+                def _():
+                    for w, go, target in ready:
+                        for i in ways[w]:
+                            go(total, target, i).start()
 
     first_row = lax.broadcasted_iota(jnp.int32, (8, nm), 0) == 0
     last_row = lax.broadcasted_iota(jnp.int32, (8, nm), 0) == 7
@@ -138,7 +175,7 @@
         src, dst = bufs[t % 2], bufs[(t + 1) % 2]
         last = t == STEPS - 1
 
-        def chunk(c, _):
+        def chunk(c, _, t=t, src=src, dst=dst, last=last):
             for side in (0, 1):
                 on(has["south"][side], lambda: x_copy(t, 1 - side, c).wait_recv())
                 on(has["down"][side], lambda: z_copy(t, 1 - side, c).wait_recv())
@@ -180,43 +217,114 @@
                 z_start(t + 1, c)
                 on(jnp.logical_and(has["east"][0], c == 0), lambda: y_copy(t + 1, 0).start())
                 on(jnp.logical_and(has["east"][1], c == chunks - 1), lambda: y_copy(t + 1, 1).start())
-            else:
-                def send_row(r, _):
-                    t_copy(c * ROWS + r).start()
-                    return 0
-
-                @pl.when(jnp.logical_not(has["south"][0]))
-                def _():
-                    lax.fori_loop(0, ROWS, send_row, 0)
             return 0
 
-        lax.fori_loop(0, chunks, chunk, 0)
-
-    @pl.when(has["south"][0])
+        if last:
+            for c in range(chunks):
+                chunk(c, 0)
+                send_totals(c)
+        else:
+            lax.fori_loop(0, chunks, chunk, 0)
+
+    def got_up(i):
+        up(total, below, i).wait_recv()
+
+    def got_down(i):
+        down(total, below, i).wait_recv()
+
+    def pairs(a, b):
+        for k in range(max(len(ways[a]), len(ways[b]))):
+            yield ways[a][k] if k < len(ways[a]) else None, ways[b][k] if k < len(ways[b]) else None
+
+    @pl.when(place["south"] == 0)
     def _():
-        def relay(i, _):
-            t_copy(i).wait_recv()
-            total[i] = total[i] + below[i]
-            on(has["south"][1], lambda: t_copy(i).start())
-            return 0
-
-        lax.fori_loop(0, ni, relay, 0)
-
-    @pl.when(jnp.logical_not(has["south"][0]))
+        for w, target in (("H", ahigh), ("B", below)):
+            for i in ways[w]:
+                got_down(i)
+                shigh[i] = total[i] + ahigh[i]
+                down(shigh, target, i).start()
+        for i in range(ni):
+            below[i] = jnp.zeros((nk, nm), jnp.float32)
+        for w in "ABH":
+            for i in ways[w]:
+                up(total, below, i).wait_send()
+        for w in "GHB":
+            for i in ways[w]:
+                down(total, below, i).wait_send()
+
+    @pl.when(place["south"] == 1)
     def _():
-        def fill(i, _):
-            below[i] = jnp.zeros((nk, nm), jnp.float32)
-            return 0
-
-        lax.fori_loop(0, ni, fill, 0)
-
-    @pl.when(has["south"][1])
+        def relay_up(i):
+            got_up(i)
+            slow[i] = below[i] + total[i]
+            up(slow, below, i).start()
+
+        for a, b in pairs("A", "B"):
+            if a is not None:
+                relay_up(a)
+            if b is not None:
+                got_down(b)
+                shigh[b] = total[b] + ahigh[b]
+                down(shigh, ahigh, b).start()
+        for i in ways["B"]:
+            relay_up(i)
+        for i in ways["G"]:
+            got_down(i)
+        for i in ways["H"]:
+            got_up(i)
+        for w in "GAB":
+            for i in ways[w]:
+                up(total, below, i).wait_send()
+        for w in "HB":
+            for i in ways[w]:
+                down(total, below, i).wait_send()
+
+    @pl.when(place["south"] == 2)
     def _():
-        def sent(i, _):
-            t_copy(i).wait_send()
-            return 0
-
-        lax.fori_loop(0, ni, sent, 0)
+        for i in ways["G"]:
+            got_up(i)
+            slow[i] = alow[i] + total[i]
+            up(slow, alow, i).start()
+        for g, a in pairs("G", "A"):
+            if g is not None:
+                got_down(g)
+                down(ahigh, below, g).start()
+                below[g] = ahigh[g] + alow[g]
+            if a is not None:
+                got_up(a)
+                slow[a] = below[a] + total[a]
+                up(slow, below, a).start()
+        for i in ways["B"]:
+            got_up(i)
+        for i in ways["H"]:
+            got_down(i)
+        for w in "HGA":
+            for i in ways[w]:
+                up(total, below, i).wait_send()
+        for w in "BG":
+            for i in ways[w]:
+                down(total, below, i).wait_send()
+
+    @pl.when(place["south"] == 3)
+    def _():
+        for i in ways["G"]:
+            got_down(i)
+            down(ahigh, ahigh, i).start()
+        for i in ways["H"]:
+            got_down(i)
+            down(ahigh, below, i).start()
+            got_up(i)
+            below[i] = ahigh[i] + alow[i]
+        for i in ways["G"]:
+            got_up(i)
+            below[i] = ahigh[i] + alow[i]
+        for i in ways["A"]:
+            got_up(i)
+        for i in ways["B"]:
+            got_down(i)
+        for w in "GH":
+            for i in ways[w]:
+                down(total, below, i).wait_send()
 
     def drain(c, _):
         for t in range(STEPS):
@@ -283,15 +391,15 @@
             pltpu.VMEM(shape, f32),
             pltpu.VMEM((STEPS, 2, ni, nj, nm), f32),
             pltpu.VMEM((STEPS, 2, ni, nj, nm), f32),
-            pltpu.VMEM((ni, nk, nm), f32),
+            *[pltpu.VMEM((ni, nk, nm), f32)] * 5,
             dma((3,)),
             dma((STEPS, 2, chunks)), dma((STEPS, 2, chunks)),
             dma((STEPS, 2)), dma((STEPS, 2)),
             dma((STEPS, 2, chunks)), dma((STEPS, 2, chunks)),
-            dma((ni,)), dma((ni,)),
+            *[dma((ni,))] * 4,
         ],
         compiler_params=pltpu.CompilerParams(
-            collective_id=0, has_side_effects=True, vmem_limit_bytes=36 * 1024 * 1024,
+            collective_id=0, has_side_effects=True, vmem_limit_bytes=40 * 1024 * 1024,
         ),
         name="steps",
     )(field_now, earlier, speed_square)

time: 131 us -> 120 us (0.916)
  Pallas kernels: 129 us -> 119 us
    pallas_call x1, Pallas kernels: 123 us -> 112 us  [shards(): pl.pallas_call(functools.partial(steps_kernel, grid_j), out_shape=(pltpu....]
where the time goes in v2:
time: 120 us; the launch traced here: 119 us
  Pallas kernels  119 us (99%)
    pallas_call x1, Pallas kernels, shards(): pl.pallas_call(functools.partial(steps_kernel, grid_j), out_shape=(pltpu....  112 us
    pallas_call x1, Pallas kernels, shards(): pl.pallas_call(functools.partial(outputs_kernel, grid_j), out_shape=(jax....  6.02 us

profile of v2, /device:TPU:103, one launch (start us, length us, event | category | flops | bytes accessed | tf_op | source)
XLA Modules:
  0.0 119.2 jit_solution(13475580979454033194)
XLA Ops:
  0.6 112.5 %steps.1 = (f32[10,18,128,128]{3,2,1,0:T(8,128)S(1)}, f32[16,128,128]{2,1,0:T(8,128)S(1)}) custom-call(f32[8,16,128,128]{3,2,1,0:T(8,128)} %u0.1, f32[8,16,128,128]{3,2,1,0:T(8,128)} %e0.1, f32[8,16,128,128]{3,2,1,0:T(8,128)} %s0.1), custom_call_target="tpu_custom_call" | custom-call | tf_op jit(solution)/shard_map/steps/pallas_call | solution.py:384
  113.1 6.0 %outputs.1 = (f32[8,16,128,128]{3,2,1,0:T(8,128)}, f32[8,16,128,128]{3,2,1,0:T(8,128)}) custom-call(f32[10,18,128,128]{3,2,1,0:T(8,128)S(1)} %get-tuple-element.4.field, f32[16,128,128]{2,1,0:T(8,128)S(1)} %get-tuple-element.5.below), custom_call_target="tpu_custom_call" | custom-call | tf_op jit(solution)/shard_map/outputs/pallas_call | solution.py:406

commit v3 on v2

--- a/solution.py
+++ b/solution.py
@@ -14,7 +14,7 @@
 
 
 def steps_kernel(
-    grid_j, u0, e0, s0, field, below, prev, speed, zsend, zrecv, total, alow, ahigh, slow, shigh,
+    grid_j, u0, e0, s0, field, below, prev, speed, zsend, zrecv, total, alow, ahigh, slow, shigh, lead,
     load_sem, xsend_sem, xrecv_sem, ysend_sem, yrecv_sem, zsend_sem, zrecv_sem, upsend_sem, uprecv_sem, downsend_sem, downrecv_sem,
 ):
     nj, ni, nk, nm = s0.shape
@@ -24,26 +24,29 @@
     has = {a: (place[a] > 0, place[a] < count[a] - 1) for a in AXES}
     peer = {a: (place[a] - 1, place[a] + 1) for a in AXES}
 
+    barrier = pltpu.get_barrier_semaphore()
+    greeted = 0
+    for a in AXES:
+        for side in (0, 1):
+            @pl.when(has[a][side])
+            def _():
+                pl.semaphore_signal(barrier, inc=1, device_id={a: peer[a][side]}, device_id_type=pl.DeviceIdType.MESH)
+            greeted = greeted + has[a][side].astype(jnp.int32)
+
     inner = (pl.ds(1, nj), pl.ds(1, ni))
+    leads = [
+        pltpu.make_async_copy(u0.at[(nj - 1) * side, pl.ds(0, ROWS)], lead.at[side], load_sem.at[3 + side]) for side in (0, 1)
+    ]
     loads = [
         pltpu.make_async_copy(u0, field.at[inner], load_sem.at[0]),
         pltpu.make_async_copy(e0, prev.at[inner], load_sem.at[1]),
         pltpu.make_async_copy(s0, speed, load_sem.at[2]),
     ]
-    for load in loads:
+    for load in leads + loads:
         load.start()
-
-    barrier = pltpu.get_barrier_semaphore()
-    greeted = 2
     ring = (lax.rem(place["south"] + count["south"] - 1, count["south"]), lax.rem(place["south"] + 1, count["south"]))
-    for side in (0, 1):
-        pl.semaphore_signal(barrier, inc=1, device_id={"south": ring[side]}, device_id_type=pl.DeviceIdType.MESH)
-    for a in AXES[1:]:
-        for side in (0, 1):
-            @pl.when(has[a][side])
-            def _():
-                pl.semaphore_signal(barrier, inc=1, device_id={a: peer[a][side]}, device_id_type=pl.DeviceIdType.MESH)
-            greeted = greeted + has[a][side].astype(jnp.int32)
+    for load in leads:
+        load.wait()
     pl.semaphore_wait(barrier, greeted)
 
     bufs = (field, prev)
@@ -82,7 +85,8 @@
     for c in range(chunks):
         rows = pl.ds(c * ROWS, ROWS)
         for side in (1, 0):
-            on(has["south"][side], lambda: x_copy(0, side, c, u0.at[nj - 1 if side else 0, rows]).start())
+            face = u0.at[nj - 1 if side else 0, rows] if c else lead.at[side]
+            on(has["south"][side], lambda: x_copy(0, side, c, face).start())
     for side in (1, 0):
         on(has["east"][side], lambda: y_copy(0, side, u0.at[:, ni - 1 if side else 0]).start())
 
@@ -392,7 +396,8 @@
             pltpu.VMEM((STEPS, 2, ni, nj, nm), f32),
             pltpu.VMEM((STEPS, 2, ni, nj, nm), f32),
             *[pltpu.VMEM((ni, nk, nm), f32)] * 5,
-            dma((3,)),
+            pltpu.VMEM((2, ROWS, nk, nm), f32),
+            dma((5,)),
             dma((STEPS, 2, chunks)), dma((STEPS, 2, chunks)),
             dma((STEPS, 2)), dma((STEPS, 2)),
             dma((STEPS, 2, chunks)), dma((STEPS, 2, chunks)),

time: 120 us -> 119 us (level)
  no operation moved by 1% of the time
where the time goes in v3:
time: 119 us
  Pallas kernels  118 us (99%)
    pallas_call x1, Pallas kernels, shards(): pl.pallas_call(functools.partial(steps_kernel, grid_j), out_shape=(pltpu....  112 us
    pallas_call x1, Pallas kernels, shards(): pl.pallas_call(functools.partial(outputs_kernel, grid_j), out_shape=(jax....  6.02 us

profile of v3, /device:TPU:103, one launch (start us, length us, event | category | flops | bytes accessed | tf_op | source)
XLA Modules:
  0.0 119.0 jit_solution(13030854746648393664)
XLA Ops:
  0.6 112.3 %steps.1 = (f32[10,18,128,128]{3,2,1,0:T(8,128)S(1)}, f32[16,128,128]{2,1,0:T(8,128)S(1)}) custom-call(f32[8,16,128,128]{3,2,1,0:T(8,128)} %u0.1, f32[8,16,128,128]{3,2,1,0:T(8,128)} %e0.1, f32[8,16,128,128]{3,2,1,0:T(8,128)} %s0.1), custom_call_target="tpu_custom_call" | custom-call | tf_op jit(solution)/shard_map/steps/pallas_call | solution.py:388
  112.9 6.0 %outputs.1 = (f32[8,16,128,128]{3,2,1,0:T(8,128)}, f32[8,16,128,128]{3,2,1,0:T(8,128)}) custom-call(f32[10,18,128,128]{3,2,1,0:T(8,128)S(1)} %get-tuple-element.4.field, f32[16,128,128]{2,1,0:T(8,128)S(1)} %get-tuple-element.5.below), custom_call_target="tpu_custom_call" | custom-call | tf_op jit(solution)/shard_map/outputs/pallas_call | solution.py:411

commit v4 on v3

--- a/solution.py
+++ b/solution.py
@@ -15,7 +15,7 @@
 
 def steps_kernel(
     grid_j, u0, e0, s0, field, below, prev, speed, zsend, zrecv, total, alow, ahigh, slow, shigh, lead,
-    load_sem, xsend_sem, xrecv_sem, ysend_sem, yrecv_sem, zsend_sem, zrecv_sem, upsend_sem, uprecv_sem, downsend_sem, downrecv_sem,
+    load_sem, xsend_sem, xrecv_sem, ysend_sem, yrecv_sem, zsend_sem, zrecv_sem, total_sem, uprecv_sem, downrecv_sem,
 ):
     nj, ni, nk, nm = s0.shape
     chunks = ni // ROWS
@@ -35,7 +35,7 @@
 
     inner = (pl.ds(1, nj), pl.ds(1, ni))
     leads = [
-        pltpu.make_async_copy(u0.at[(nj - 1) * side, pl.ds(0, ROWS)], lead.at[side], load_sem.at[3 + side]) for side in (0, 1)
+        pltpu.make_async_copy(u0.at[(nj - 1) * side, pl.ds(0, ROWS)], lead.at[side], load_sem.at[3]) for side in (0, 1)
     ]
     loads = [
         pltpu.make_async_copy(u0, field.at[inner], load_sem.at[0]),
@@ -45,8 +45,7 @@
     for load in leads + loads:
         load.start()
     ring = (lax.rem(place["south"] + count["south"] - 1, count["south"]), lax.rem(place["south"] + 1, count["south"]))
-    for load in leads:
-        load.wait()
+    pltpu.make_async_copy(u0.at[pl.ds(0, 2), pl.ds(0, ROWS)], lead, load_sem.at[3]).wait()
     pl.semaphore_wait(barrier, greeted)
 
     bufs = (field, prev)
@@ -62,20 +61,35 @@
         rows = pl.ds(1 + c * ROWS, ROWS)
         own, dst = (nj if side else 1), (0 if side else nj + 1)
         src = buf.at[own, rows] if src is None else src
-        return remote(src, buf.at[dst, rows], xsend_sem.at[t, side, c], xrecv_sem.at[t, 1 - side, c], "south", side)
+        return remote(src, buf.at[dst, rows], xsend_sem.at[t % 2, side], xrecv_sem.at[t % 2, c], "south", side)
 
     def y_copy(t, side, src=None):
         buf = bufs[t % 2]
         own, dst = (ni if side else 1), (0 if side else ni + 1)
         src = buf.at[pl.ds(1, nj), own] if src is None else src
-        return remote(src, buf.at[pl.ds(1, nj), dst], ysend_sem.at[t, side], yrecv_sem.at[t, 1 - side], "east", side)
+        return remote(src, buf.at[pl.ds(1, nj), dst], ysend_sem.at[t % 2, side], yrecv_sem.at[t % 2, 1 - side], "east", side)
 
     def z_copy(t, side, c):
         rows = pl.ds(c * ROWS, ROWS)
         return remote(
             zsend.at[t, side, rows], zrecv.at[t, 1 - side, rows],
-            zsend_sem.at[t, side, c], zrecv_sem.at[t, 1 - side, c], "down", side,
+            zsend_sem.at[side], zrecv_sem.at[t % 2, c], "down", side,
         )
+
+    def arrived(axis, sem, one, both):
+        two = jnp.logical_and(*has[axis])
+        for pred, ref in ((two, both), (jnp.logical_not(two), one)):
+            @pl.when(pred)
+            def _():
+                remote(ref, ref, zsend_sem.at[0], sem, axis, 0).wait_recv()
+
+    def sent(axis, sems, ref):
+        for side in (0, 1):
+            on(has[axis][side], lambda: remote(ref, ref, sems(side), zrecv_sem.at[0, 0], axis, side).wait_send())
+
+    def sent_faces(t):
+        sent("south", lambda side: xsend_sem.at[t % 2, side], field.at[0, pl.ds(1, ni)])
+        sent("east", lambda side: ysend_sem.at[t % 2, side], field.at[pl.ds(1, nj), 0])
 
     def on(pred, action):
         @pl.when(pred)
@@ -136,19 +150,29 @@
     loads[1].wait()
     loads[2].wait()
 
-    def up(src, dst, i):
+    ways = {w: [c * ROWS + r for c in cs for r in range(ROWS)] for w, cs in WAYS.items()}
+    came = {"up": {1: "ABH", 2: "GAB", 3: "HGA"}, "down": {0: "HB", 1: "BG", 2: "GH", 3: "GHB"}}
+    slot = {(key, x): [i for w in ws for i in ways[w]].index for key, at in came.items() for x, ws in at.items()}
+
+    def up(src, dst, i, x):
         return pltpu.make_async_remote_copy(
-            src_ref=src.at[i], dst_ref=dst.at[i], send_sem=upsend_sem.at[i], recv_sem=uprecv_sem.at[i],
+            src_ref=src.at[i], dst_ref=dst.at[i], send_sem=total_sem.at[0], recv_sem=uprecv_sem.at[slot["up", x + 1](i)],
             device_id={"south": ring[1]}, device_id_type=pl.DeviceIdType.MESH,
         )
 
-    def down(src, dst, i):
+    def down(src, dst, i, x):
         return pltpu.make_async_remote_copy(
-            src_ref=src.at[i], dst_ref=dst.at[i], send_sem=downsend_sem.at[i], recv_sem=downrecv_sem.at[i],
+            src_ref=src.at[i], dst_ref=dst.at[i], send_sem=total_sem.at[1], recv_sem=downrecv_sem.at[slot["down", (x + 3) % 4](i)],
             device_id={"south": ring[0]}, device_id_type=pl.DeviceIdType.MESH,
         )
 
-    ways = {w: [c * ROWS + r for c in cs for r in range(ROWS)] for w, cs in WAYS.items()}
+    def totals_sent(side, n):
+        ref = total.at[pl.ds(0, n)]
+        pltpu.make_async_remote_copy(
+            src_ref=ref, dst_ref=ref, send_sem=total_sem.at[side], recv_sem=uprecv_sem.at[0],
+            device_id={"south": ring[1 - side]}, device_id_type=pl.DeviceIdType.MESH,
+        ).wait_send()
+
     first = {
         0: (("G", down, ahigh), ("A", up, below), ("B", up, below), ("H", up, below)),
         1: (("G", up, alow), ("H", down, ahigh)),
@@ -170,7 +194,7 @@
                 def _():
                     for w, go, target in ready:
                         for i in ways[w]:
-                            go(total, target, i).start()
+                            go(total, target, i, x).start()
 
     first_row = lax.broadcasted_iota(jnp.int32, (8, nm), 0) == 0
     last_row = lax.broadcasted_iota(jnp.int32, (8, nm), 0) == 7
@@ -180,16 +204,12 @@
         last = t == STEPS - 1
 
         def chunk(c, _, t=t, src=src, dst=dst, last=last):
-            for side in (0, 1):
-                on(has["south"][side], lambda: x_copy(t, 1 - side, c).wait_recv())
-                on(has["down"][side], lambda: z_copy(t, 1 - side, c).wait_recv())
+            buf = bufs[t % 2]
+            arrived("south", xrecv_sem.at[t % 2, c], buf.at[0, pl.ds(1, ROWS)], buf.at[0, pl.ds(1, 2 * ROWS)])
+            rows = pl.ds(c * ROWS, ROWS)
+            arrived("down", zrecv_sem.at[t % 2, c], zrecv.at[t, 0, rows], zrecv.at[t, pl.ds(0, 2), rows])
             on(jnp.logical_and(has["east"][0], c == 0), lambda: y_copy(t, 1).wait_recv())
             on(jnp.logical_and(has["east"][1], c == chunks - 1), lambda: y_copy(t, 0).wait_recv())
-            if t >= 2:
-                for side in (0, 1):
-                    on(has["south"][side], lambda: x_copy(t - 1, side, c).wait_send())
-                on(jnp.logical_and(has["east"][0], c == 0), lambda: y_copy(t - 1, 0).wait_send())
-                on(jnp.logical_and(has["east"][1], c == chunks - 1), lambda: y_copy(t - 1, 1).wait_send())
 
             def row(r, _):
                 i = c * ROWS + r
@@ -223,6 +243,8 @@
                 on(jnp.logical_and(has["east"][1], c == chunks - 1), lambda: y_copy(t + 1, 1).start())
             return 0
 
+        if t >= 1:
+            sent_faces(t - 1)
         if last:
             for c in range(chunks):
                 chunk(c, 0)
@@ -230,11 +252,11 @@
         else:
             lax.fori_loop(0, chunks, chunk, 0)
 
-    def got_up(i):
-        up(total, below, i).wait_recv()
-
-    def got_down(i):
-        down(total, below, i).wait_recv()
+    def got_up(i, x):
+        up(total, below, i, x - 1).wait_recv()
+
+    def got_down(i, x):
+        down(total, below, i, (x + 1) % 4).wait_recv()
 
     def pairs(a, b):
         for k in range(max(len(ways[a]), len(ways[b]))):
@@ -244,104 +266,82 @@
     def _():
         for w, target in (("H", ahigh), ("B", below)):
             for i in ways[w]:
-                got_down(i)
+                got_down(i, 0)
                 shigh[i] = total[i] + ahigh[i]
-                down(shigh, target, i).start()
+                down(shigh, target, i, 0).start()
         for i in range(ni):
             below[i] = jnp.zeros((nk, nm), jnp.float32)
-        for w in "ABH":
-            for i in ways[w]:
-                up(total, below, i).wait_send()
-        for w in "GHB":
-            for i in ways[w]:
-                down(total, below, i).wait_send()
+        totals_sent(0, sum(len(ways[w]) for w in "ABH"))
+        totals_sent(1, sum(len(ways[w]) for w in "GHB"))
 
     @pl.when(place["south"] == 1)
     def _():
         def relay_up(i):
-            got_up(i)
+            got_up(i, 1)
             slow[i] = below[i] + total[i]
-            up(slow, below, i).start()
+            up(slow, below, i, 1).start()
 
         for a, b in pairs("A", "B"):
             if a is not None:
                 relay_up(a)
             if b is not None:
-                got_down(b)
+                got_down(b, 1)
                 shigh[b] = total[b] + ahigh[b]
-                down(shigh, ahigh, b).start()
+                down(shigh, ahigh, b, 1).start()
         for i in ways["B"]:
             relay_up(i)
         for i in ways["G"]:
-            got_down(i)
+            got_down(i, 1)
         for i in ways["H"]:
-            got_up(i)
-        for w in "GAB":
-            for i in ways[w]:
-                up(total, below, i).wait_send()
-        for w in "HB":
-            for i in ways[w]:
-                down(total, below, i).wait_send()
+            got_up(i, 1)
+        totals_sent(0, sum(len(ways[w]) for w in "GAB"))
+        totals_sent(1, sum(len(ways[w]) for w in "HB"))
 
     @pl.when(place["south"] == 2)
     def _():
         for i in ways["G"]:
-            got_up(i)
+            got_up(i, 2)
             slow[i] = alow[i] + total[i]
-            up(slow, alow, i).start()
+            up(slow, alow, i, 2).start()
         for g, a in pairs("G", "A"):
             if g is not None:
-                got_down(g)
-                down(ahigh, below, g).start()
+                got_down(g, 2)
+                down(ahigh, below, g, 2).start()
                 below[g] = ahigh[g] + alow[g]
             if a is not None:
-                got_up(a)
+                got_up(a, 2)
                 slow[a] = below[a] + total[a]
-                up(slow, below, a).start()
+                up(slow, below, a, 2).start()
         for i in ways["B"]:
-            got_up(i)
+            got_up(i, 2)
         for i in ways["H"]:
-            got_down(i)
-        for w in "HGA":
-            for i in ways[w]:
-                up(total, below, i).wait_send()
-        for w in "BG":
-            for i in ways[w]:
-                down(total, below, i).wait_send()
+            got_down(i, 2)
+        totals_sent(0, sum(len(ways[w]) for w in "HGA"))
+        totals_sent(1, sum(len(ways[w]) for w in "BG"))
 
     @pl.when(place["south"] == 3)
     def _():
         for i in ways["G"]:
-            got_down(i)
-            down(ahigh, ahigh, i).start()
+            got_down(i, 3)
+            down(ahigh, ahigh, i, 3).start()
         for i in ways["H"]:
-            got_down(i)
-            down(ahigh, below, i).start()
-            got_up(i)
+            got_down(i, 3)
+            down(ahigh, below, i, 3).start()
+            got_up(i, 3)
             below[i] = ahigh[i] + alow[i]
         for i in ways["G"]:
-            got_up(i)
+            got_up(i, 3)
             below[i] = ahigh[i] + alow[i]
         for i in ways["A"]:
-            got_up(i)
+            got_up(i, 3)
         for i in ways["B"]:
-            got_down(i)
-        for w in "GH":
-            for i in ways[w]:
-                down(total, below, i).wait_send()
-
-    def drain(c, _):
-        for t in range(STEPS):
-            for side in (0, 1):
-                if t in (0, STEPS - 1):
-                    on(has["south"][side], lambda: x_copy(t, side, c).wait_send())
-                on(has["down"][side], lambda: z_copy(t, side, c).wait_send())
-        return 0
-
-    lax.fori_loop(0, chunks, drain, 0)
-    for t in (0, STEPS - 1):
-        for side in (0, 1):
-            on(has["east"][side], lambda: y_copy(t, side).wait_send())
+            got_down(i, 3)
+        totals_sent(1, sum(len(ways[w]) for w in "GH"))
+
+    sent_faces(STEPS - 1)
+    for side in (0, 1):
+        ref = zsend.at[:, side]
+        on(has["down"][side], lambda: remote(ref, ref, zsend_sem.at[side], zrecv_sem.at[0, 0], "down", side).wait_send())
 
 
 def outputs_kernel(grid_j, field, below, running, end, stage, out_sem, field_sem):
@@ -353,7 +353,7 @@
 
     def out(g):
         at = pl.ds(g * rows, rows)
-        return pltpu.make_async_copy(stage.at[:, at], running.at[:, at], out_sem.at[g])
+        return pltpu.make_async_copy(stage.at[:, at], running.at[:, at], out_sem)
 
     def group(g, _):
         for r in range(rows):
@@ -367,11 +367,7 @@
 
     lax.fori_loop(0, groups, group, 0)
 
-    def done(g, _):
-        out(g).wait()
-        return 0
-
-    lax.fori_loop(0, groups, done, 0)
+    pltpu.make_async_copy(stage, running, out_sem).wait()
     whole.wait()
 
 
@@ -397,11 +393,11 @@
             pltpu.VMEM((STEPS, 2, ni, nj, nm), f32),
             *[pltpu.VMEM((ni, nk, nm), f32)] * 5,
             pltpu.VMEM((2, ROWS, nk, nm), f32),
-            dma((5,)),
-            dma((STEPS, 2, chunks)), dma((STEPS, 2, chunks)),
-            dma((STEPS, 2)), dma((STEPS, 2)),
-            dma((STEPS, 2, chunks)), dma((STEPS, 2, chunks)),
-            *[dma((ni,))] * 4,
+            dma((4,)),
+            dma((2, 2)), dma((2, chunks)),
+            dma((2, 2)), dma((2, 2)),
+            dma((2,)), dma((2, chunks)),
+            dma((2,)), dma((3 * ni // 4,)), dma((3 * ni // 4,)),
         ],
         compiler_params=pltpu.CompilerParams(
             collective_id=0, has_side_effects=True, vmem_limit_bytes=40 * 1024 * 1024,
@@ -413,7 +409,7 @@
         out_shape=(jax.ShapeDtypeStruct(shape, f32), jax.ShapeDtypeStruct(shape, f32)),
         in_specs=[vmem, vmem],
         out_specs=(anyspace, anyspace),
-        scratch_shapes=[pltpu.VMEM(shape, f32), dma((ni // 2,)), dma],
+        scratch_shapes=[pltpu.VMEM(shape, f32), dma, dma],
         compiler_params=pltpu.CompilerParams(vmem_limit_bytes=32 * 1024 * 1024),
         name="outputs",
     )(field, below)

time: 119 us -> 118 us (level)
    pallas_call x1, Pallas kernels: 112 us -> 111 us  [shards(): pl.pallas_call(functools.partial(steps_kernel, grid_j), out_shape=(pltpu....]
where the time goes in v4:
time: 118 us; the launch traced here: 117 us
  Pallas kernels  117 us (99%)
    pallas_call x1, Pallas kernels, shards(): pl.pallas_call(functools.partial(steps_kernel, grid_j), out_shape=(pltpu....  111 us
    pallas_call x1, Pallas kernels, shards(): pl.pallas_call(functools.partial(outputs_kernel, grid_j), out_shape=(jax....  5.96 us

profile of v4, /device:TPU:103, one launch (start us, length us, event | category | flops | bytes accessed | tf_op | source)
XLA Modules:
  0.0 117.5 jit_solution(17185477582641780254)
XLA Ops:
  0.6 110.9 %steps.1 = (f32[10,18,128,128]{3,2,1,0:T(8,128)S(1)}, f32[16,128,128]{2,1,0:T(8,128)S(1)}) custom-call(f32[8,16,128,128]{3,2,1,0:T(8,128)} %u0.1, f32[8,16,128,128]{3,2,1,0:T(8,128)} %e0.1, f32[8,16,128,128]{3,2,1,0:T(8,128)} %s0.1), custom_call_target="tpu_custom_call" | custom-call | tf_op jit(solution)/shard_map/steps/pallas_call | solution.py:384
  111.5 6.0 %outputs.1 = (f32[8,16,128,128]{3,2,1,0:T(8,128)}, f32[8,16,128,128]{3,2,1,0:T(8,128)}) custom-call(f32[10,18,128,128]{3,2,1,0:T(8,128)S(1)} %get-tuple-element.4.field, f32[16,128,128]{2,1,0:T(8,128)S(1)} %get-tuple-element.5.below), custom_call_target="tpu_custom_call" | custom-call | tf_op jit(solution)/shard_map/outputs/pallas_call | solution.py:407

commit v5 on v4

--- a/solution.py
+++ b/solution.py
@@ -25,13 +25,17 @@
     peer = {a: (place[a] - 1, place[a] + 1) for a in AXES}
 
     barrier = pltpu.get_barrier_semaphore()
-    greeted = 0
-    for a in AXES:
+
+    def greet(a):
         for side in (0, 1):
             @pl.when(has[a][side])
             def _():
                 pl.semaphore_signal(barrier, inc=1, device_id={a: peer[a][side]}, device_id_type=pl.DeviceIdType.MESH)
-            greeted = greeted + has[a][side].astype(jnp.int32)
+        return has[a][0].astype(jnp.int32) + has[a][1].astype(jnp.int32)
+
+    odd = lax.rem(place["east"], 2) == 1
+    greeted = greet("south") + greet("down")
+    beside = has["east"][0].astype(jnp.int32) + has["east"][1].astype(jnp.int32)
 
     inner = (pl.ds(1, nj), pl.ds(1, ni))
     leads = [
@@ -46,7 +50,8 @@
         load.start()
     ring = (lax.rem(place["south"] + count["south"] - 1, count["south"]), lax.rem(place["south"] + 1, count["south"]))
     pltpu.make_async_copy(u0.at[pl.ds(0, 2), pl.ds(0, ROWS)], lead, load_sem.at[3]).wait()
-    pl.semaphore_wait(barrier, greeted)
+    pl.semaphore_wait(barrier, greeted + jnp.where(odd, 0, beside))
+    greet("east")
 
     bufs = (field, prev)
 
@@ -101,6 +106,7 @@
         for side in (1, 0):
             face = u0.at[nj - 1 if side else 0, rows] if c else lead.at[side]
             on(has["south"][side], lambda: x_copy(0, side, c, face).start())
+    on(odd, lambda: pl.semaphore_wait(barrier, beside))
     for side in (1, 0):
         on(has["east"][side], lambda: y_copy(0, side, u0.at[:, ni - 1 if side else 0]).start())
 

time: 118 us -> 117 us (level)
  Pallas kernels: 117 us -> 115 us
    pallas_call x1, Pallas kernels: 111 us -> 109 us  [shards(): pl.pallas_call(functools.partial(steps_kernel, grid_j), out_shape=(pltpu....]
where the time goes in v5:
time: 117 us; the launch traced here: 116 us
  Pallas kernels  115 us (98%)
    pallas_call x1, Pallas kernels, shards(): pl.pallas_call(functools.partial(steps_kernel, grid_j), out_shape=(pltpu....  109 us
    pallas_call x1, Pallas kernels, shards(): pl.pallas_call(functools.partial(outputs_kernel, grid_j), out_shape=(jax....  5.96 us

profile of v5, /device:TPU:103, one launch (start us, length us, event | category | flops | bytes accessed | tf_op | source)
XLA Modules:
  0.0 115.8 jit_solution(14352410199033184658)
XLA Ops:
  0.6 109.2 %steps.1 = (f32[10,18,128,128]{3,2,1,0:T(8,128)S(1)}, f32[16,128,128]{2,1,0:T(8,128)S(1)}) custom-call(f32[8,16,128,128]{3,2,1,0:T(8,128)} %u0.1, f32[8,16,128,128]{3,2,1,0:T(8,128)} %e0.1, f32[8,16,128,128]{3,2,1,0:T(8,128)} %s0.1), custom_call_target="tpu_custom_call" | custom-call | tf_op jit(solution)/shard_map/steps/pallas_call | solution.py:390
  109.9 6.0 %outputs.1 = (f32[8,16,128,128]{3,2,1,0:T(8,128)}, f32[8,16,128,128]{3,2,1,0:T(8,128)}) custom-call(f32[10,18,128,128]{3,2,1,0:T(8,128)S(1)} %get-tuple-element.4.field, f32[16,128,128]{2,1,0:T(8,128)S(1)} %get-tuple-element.5.below), custom_call_target="tpu_custom_call" | custom-call | tf_op jit(solution)/shard_map/outputs/pallas_call | solution.py:413

commit v6 on v5

--- a/solution.py
+++ b/solution.py
@@ -10,7 +10,21 @@
 STEPS = 4
 ROWS = 4
 AXES = ("south", "east", "down")
-WAYS = {"G": (0,), "H": (1,), "A": (2,), "B": (3,)}
+
+TABLES = (
+    (
+        "GHBHAGAGHBGABBHA",
+        {(0, "up"): (8, 6, 11, 4, 12, 15, 13, 2, 9, 3, 14, 1), (0, "down"): (7, 0, 5, 10), (1, "up"): (5, 7, 10, 0), (1, "down"): (8, 1, 3, 14), (2, "up"): (3, 8, 1, 14), (2, "down"): (2, 9, 12, 13)},
+        {0: ((-1, 8), (-1, 1), (-1, 3), (-1, 14), (-1, 2), (-1, 9), (-1, 12), (-1, 13)), 1: ((-1, 2), (1, 6), (-1, 9), (1, 11), (-1, 12), (1, 4), (-1, 13), (1, 12), (1, 15), (1, 13), (1, 2), (1, 9)), 2: ((1, 5), (1, 7), (1, 10), (-1, 7), (1, 0), (-1, 0), (1, 6), (-1, 5), (1, 11), (-1, 10), (1, 4), (1, 15)), 3: ((-1, 7), (-1, 0), (-1, 5), (-1, 10), (-1, 8), (-1, 1), (-1, 3), (-1, 14))},
+    ),
+    (
+        "HGGBBGGBHGHBHAAB",
+        {(0, "up"): (4, 8, 10, 14, 7, 13, 15, 3, 11, 12, 0), (0, "down"): (2, 9, 1, 6, 5), (1, "up"): (6, 5, 2, 1, 9), (1, "down"): (0, 10, 8, 12), (2, "up"): (0, 8, 10, 12), (2, "down"): (11, 7, 3, 15, 4)},
+        {0: ((-1, 0), (-1, 10), (-1, 8), (-1, 12), (-1, 11), (-1, 7), (-1, 3), (-1, 15), (-1, 4)), 1: ((1, 4), (-1, 11), (-1, 7), (-1, 3), (1, 14), (-1, 15), (1, 7), (-1, 4), (1, 13), (1, 15), (1, 3), (1, 11)), 2: ((1, 6), (1, 5), (1, 2), (-1, 2), (1, 1), (-1, 9), (1, 9), (-1, 1), (-1, 6), (1, 14), (-1, 5), (1, 13)), 3: ((-1, 2), (-1, 9), (-1, 1), (-1, 6), (-1, 5), (-1, 0), (-1, 10), (-1, 8), (-1, 12))},
+    ),
+)
+ENDS = {0: [], 1: [("down", "G"), ("up", "H")], 2: [("down", "H"), ("up", "B")], 3: [("up", "H"), ("up", "G"), ("down", "B"), ("up", "A")]}
+PLAIN = {(1, "up"): "ABH", (2, "up"): "AB", (3, "up"): "A", (1, "down"): "G", (2, "down"): "H", (3, "down"): "B", (0, "down"): ""}
 
 
 def steps_kernel(
@@ -156,51 +170,51 @@
     loads[1].wait()
     loads[2].wait()
 
-    ways = {w: [c * ROWS + r for c in cs for r in range(ROWS)] for w, cs in WAYS.items()}
-    came = {"up": {1: "ABH", 2: "GAB", 3: "HGA"}, "down": {0: "HB", 1: "BG", 2: "GH", 3: "GHB"}}
-    slot = {(key, x): [i for w in ws for i in ways[w]].index for key, at in came.items() for x, ws in at.items()}
-
-    def up(src, dst, i, x):
+    recv = {"up": uprecv_sem, "down": downrecv_sem}
+
+    def landing(x, way, w):
+        return below if w in PLAIN[x, way] else (alow if way == "up" else ahigh)
+
+    relays = [
+        {x: [("up" if e > 0 else "down", i) for e, i in line] for x, line in table[2].items()} for table in TABLES
+    ]
+    slots = [{}, {}]
+    for p in (0, 1):
+        for x in range(4):
+            for way in ("up", "down"):
+                here = [i for k, i in relays[p][x] if k == way] + [w for k, w in ENDS[x] if k == way]
+                slots[p].update({(x, way, key): n for n, key in enumerate(here)})
+
+    def ring_copy(way, src, dst, recv_sem):
         return pltpu.make_async_remote_copy(
-            src_ref=src.at[i], dst_ref=dst.at[i], send_sem=total_sem.at[0], recv_sem=uprecv_sem.at[slot["up", x + 1](i)],
-            device_id={"south": ring[1]}, device_id_type=pl.DeviceIdType.MESH,
+            src_ref=src, dst_ref=dst, send_sem=total_sem.at[int(way == "down")], recv_sem=recv_sem,
+            device_id={"south": ring[int(way == "up")]}, device_id_type=pl.DeviceIdType.MESH,
         )
 
-    def down(src, dst, i, x):
-        return pltpu.make_async_remote_copy(
-            src_ref=src.at[i], dst_ref=dst.at[i], send_sem=total_sem.at[1], recv_sem=downrecv_sem.at[slot["down", (x + 3) % 4](i)],
-            device_id={"south": ring[0]}, device_id_type=pl.DeviceIdType.MESH,
-        )
-
-    def totals_sent(side, n):
-        ref = total.at[pl.ds(0, n)]
-        pltpu.make_async_remote_copy(
-            src_ref=ref, dst_ref=ref, send_sem=total_sem.at[side], recv_sem=uprecv_sem.at[0],
-            device_id={"south": ring[1 - side]}, device_id_type=pl.DeviceIdType.MESH,
-        ).wait_send()
-
-    first = {
-        0: (("G", down, ahigh), ("A", up, below), ("B", up, below), ("H", up, below)),
-        1: (("G", up, alow), ("H", down, ahigh)),
-        2: (("H", up, alow), ("B", down, ahigh)),
-        3: (),
-    }
+    def pass_on(p, x, way, i, src):
+        to = (x + (1 if way == "up" else 3)) % 4
+        w = TABLES[p][0][i]
+        slot = slots[p][to, way, i] if (to, way, i) in slots[p] else slots[p][to, way, w]
+        ring_copy(way, src.at[i], landing(to, way, w).at[i], recv[way].at[slot]).start()
+
+    def here(p, x):
+        return jnp.logical_and(odd == bool(p), place["south"] == x)
 
     def send_totals(c):
-        for x, sends in first.items():
-            ready = []
-            latest = {"up": 0, "down": 0}
-            for w, go, target in sends:
-                key = "up" if go is up else "down"
-                latest[key] = max(latest[key], max(WAYS[w]))
-                if latest[key] == c:
-                    ready.append((w, go, target))
-            if ready:
-                @pl.when(place["south"] == x)
-                def _():
-                    for w, go, target in ready:
-                        for i in ways[w]:
-                            go(total, target, i, x).start()
+        for p in (0, 1):
+            for x in range(3):
+                ready = []
+                for way in ("up", "down"):
+                    latest = 0
+                    for i in TABLES[p][1][x, way]:
+                        latest = max(latest, i // ROWS)
+                        if latest == c:
+                            ready.append((way, i))
+                if ready:
+                    @pl.when(here(p, x))
+                    def _():
+                        for way, i in ready:
+                            pass_on(p, x, way, i, total)
 
     first_row = lax.broadcasted_iota(jnp.int32, (8, nm), 0) == 0
     last_row = lax.broadcasted_iota(jnp.int32, (8, nm), 0) == 7
@@ -258,91 +272,38 @@
         else:
             lax.fori_loop(0, chunks, chunk, 0)
 
-    def got_up(i, x):
-        up(total, below, i, x - 1).wait_recv()
-
-    def got_down(i, x):
-        down(total, below, i, (x + 1) % 4).wait_recv()
-
-    def pairs(a, b):
-        for k in range(max(len(ways[a]), len(ways[b]))):
-            yield ways[a][k] if k < len(ways[a]) else None, ways[b][k] if k < len(ways[b]) else None
-
-    @pl.when(place["south"] == 0)
-    def _():
-        for w, target in (("H", ahigh), ("B", below)):
-            for i in ways[w]:
-                got_down(i, 0)
-                shigh[i] = total[i] + ahigh[i]
-                down(shigh, target, i, 0).start()
-        for i in range(ni):
-            below[i] = jnp.zeros((nk, nm), jnp.float32)
-        totals_sent(0, sum(len(ways[w]) for w in "ABH"))
-        totals_sent(1, sum(len(ways[w]) for w in "GHB"))
-
-    @pl.when(place["south"] == 1)
-    def _():
-        def relay_up(i):
-            got_up(i, 1)
-            slow[i] = below[i] + total[i]
-            up(slow, below, i, 1).start()
-
-        for a, b in pairs("A", "B"):
-            if a is not None:
-                relay_up(a)
-            if b is not None:
-                got_down(b, 1)
-                shigh[b] = total[b] + ahigh[b]
-                down(shigh, ahigh, b, 1).start()
-        for i in ways["B"]:
-            relay_up(i)
-        for i in ways["G"]:
-            got_down(i, 1)
-        for i in ways["H"]:
-            got_up(i, 1)
-        totals_sent(0, sum(len(ways[w]) for w in "GAB"))
-        totals_sent(1, sum(len(ways[w]) for w in "HB"))
-
-    @pl.when(place["south"] == 2)
-    def _():
-        for i in ways["G"]:
-            got_up(i, 2)
-            slow[i] = alow[i] + total[i]
-            up(slow, alow, i, 2).start()
-        for g, a in pairs("G", "A"):
-            if g is not None:
-                got_down(g, 2)
-                down(ahigh, below, g, 2).start()
-                below[g] = ahigh[g] + alow[g]
-            if a is not None:
-                got_up(a, 2)
-                slow[a] = below[a] + total[a]
-                up(slow, below, a, 2).start()
-        for i in ways["B"]:
-            got_up(i, 2)
-        for i in ways["H"]:
-            got_down(i, 2)
-        totals_sent(0, sum(len(ways[w]) for w in "HGA"))
-        totals_sent(1, sum(len(ways[w]) for w in "BG"))
-
-    @pl.when(place["south"] == 3)
-    def _():
-        for i in ways["G"]:
-            got_down(i, 3)
-            down(ahigh, ahigh, i, 3).start()
-        for i in ways["H"]:
-            got_down(i, 3)
-            down(ahigh, below, i, 3).start()
-            got_up(i, 3)
-            below[i] = ahigh[i] + alow[i]
-        for i in ways["G"]:
-            got_up(i, 3)
-            below[i] = ahigh[i] + alow[i]
-        for i in ways["A"]:
-            got_up(i, 3)
-        for i in ways["B"]:
-            got_down(i, 3)
-        totals_sent(1, sum(len(ways[w]) for w in "GH"))
+    for p, x in [(p, x) for p in (0, 1) for x in range(4)]:
+        @pl.when(here(p, x))
+        def _():
+            ways, own, _ = TABLES[p]
+            for way, i in relays[p][x]:
+                came = landing(x, way, ways[i])
+                ring_copy(way, came.at[i], came.at[i], recv[way].at[slots[p][x, way, i]]).wait_recv()
+                if x == 3 or (x, way) == (2, "down"):
+                    pass_on(p, x, way, i, came)
+                else:
+                    out = slow if way == "up" else shigh
+                    out[i] = came[i] + total[i]
+                    pass_on(p, x, way, i, out)
+            if x == 2:
+                for i in range(ni):
+                    if ways[i] == "G":
+                        below[i] = ahigh[i] + alow[i]
+            for way, w in ENDS[x]:
+                rows = [i for i in range(ni) if ways[i] == w]
+                ref = total.at[pl.ds(0, len(rows))]
+                ring_copy(way, ref, ref, recv[way].at[slots[p][x, way, w]]).wait_recv()
+                if landing(x, way, w) is not below:
+                    for i in rows:
+                        below[i] = ahigh[i] + alow[i]
+            if x == 0:
+                for i in range(ni):
+                    below[i] = jnp.zeros((nk, nm), jnp.float32)
+            for way in ("up", "down"):
+                count = len(own.get((x, way), ())) + sum(k == way for k, _ in relays[p][x])
+                if count:
+                    ref = total.at[pl.ds(0, count)]
+                    ring_copy(way, ref, ref, uprecv_sem.at[0]).wait_send()
 
     sent_faces(STEPS - 1)
     for side in (0, 1):
@@ -403,7 +364,7 @@
             dma((2, 2)), dma((2, chunks)),
             dma((2, 2)), dma((2, 2)),
             dma((2,)), dma((2, chunks)),
-            dma((2,)), dma((3 * ni // 4,)), dma((3 * ni // 4,)),
+            dma((2,)), dma((9,)), dma((11,)),
         ],
         compiler_params=pltpu.CompilerParams(
             collective_id=0, has_side_effects=True, vmem_limit_bytes=40 * 1024 * 1024,

time: 117 us -> 117 us (level)
  no operation moved by 1% of the time
where the time goes in v6:
time: 117 us; the launch traced here: 115 us
  Pallas kernels  114 us (97%)
    pallas_call x1, Pallas kernels, shards(): pl.pallas_call(functools.partial(steps_kernel, grid_j), out_shape=(pltpu....  108 us
    pallas_call x1, Pallas kernels, shards(): pl.pallas_call(functools.partial(outputs_kernel, grid_j), out_shape=(jax....  5.96 us

profile of v6, /device:TPU:103, one launch (start us, length us, event | category | flops | bytes accessed | tf_op | source)
XLA Modules:
  0.0 115.1 jit_solution(13852596452855402976)
XLA Ops:
  0.6 108.5 %steps.1 = (f32[10,18,128,128]{3,2,1,0:T(8,128)S(1)}, f32[16,128,128]{2,1,0:T(8,128)S(1)}) custom-call(f32[8,16,128,128]{3,2,1,0:T(8,128)} %u0.1, f32[8,16,128,128]{3,2,1,0:T(8,128)} %e0.1, f32[8,16,128,128]{3,2,1,0:T(8,128)} %s0.1), custom_call_target="tpu_custom_call" | custom-call | tf_op jit(solution)/shard_map/steps/pallas_call | solution.py:351
  109.1 6.0 %outputs.1 = (f32[8,16,128,128]{3,2,1,0:T(8,128)}, f32[8,16,128,128]{3,2,1,0:T(8,128)}) custom-call(f32[10,18,128,128]{3,2,1,0:T(8,128)S(1)} %get-tuple-element.4.field, f32[16,128,128]{2,1,0:T(8,128)S(1)} %get-tuple-element.5.below), custom_call_target="tpu_custom_call" | custom-call | tf_op jit(solution)/shard_map/outputs/pallas_call | solution.py:374

commit v7 on v6

--- a/solution.py
+++ b/solution.py
@@ -13,14 +13,14 @@
 
 TABLES = (
     (
-        "GHBHAGAGHBGABBHA",
-        {(0, "up"): (8, 6, 11, 4, 12, 15, 13, 2, 9, 3, 14, 1), (0, "down"): (7, 0, 5, 10), (1, "up"): (5, 7, 10, 0), (1, "down"): (8, 1, 3, 14), (2, "up"): (3, 8, 1, 14), (2, "down"): (2, 9, 12, 13)},
-        {0: ((-1, 8), (-1, 1), (-1, 3), (-1, 14), (-1, 2), (-1, 9), (-1, 12), (-1, 13)), 1: ((-1, 2), (1, 6), (-1, 9), (1, 11), (-1, 12), (1, 4), (-1, 13), (1, 12), (1, 15), (1, 13), (1, 2), (1, 9)), 2: ((1, 5), (1, 7), (1, 10), (-1, 7), (1, 0), (-1, 0), (1, 6), (-1, 5), (1, 11), (-1, 10), (1, 4), (1, 15)), 3: ((-1, 7), (-1, 0), (-1, 5), (-1, 10), (-1, 8), (-1, 1), (-1, 3), (-1, 14))},
+        "HBBGGGHGHAAGABBH",
+        {(0, "up"): (0, 8, 9, 10, 13, 12, 1, 2, 14, 6, 15), (0, "down"): (7, 4, 5, 3, 11), (1, "up"): (3, 5, 4, 11, 7), (1, "down"): (8, 6, 0, 15), (2, "up"): (6, 0, 8, 15), (2, "down"): (2, 13, 1, 14)},
+        {0: ((-1, 8), (-1, 6), (-1, 0), (-1, 15), (-1, 2), (-1, 13), (-1, 1), (-1, 14)), 1: ((-1, 2), (1, 9), (-1, 13), (1, 10), (-1, 1), (1, 13), (-1, 14), (1, 12), (1, 1), (1, 2), (1, 14)), 2: ((1, 3), (1, 5), (1, 4), (-1, 7), (1, 11), (-1, 4), (1, 7), (-1, 5), (1, 9), (-1, 3), (1, 10), (-1, 11), (1, 12)), 3: ((-1, 7), (-1, 4), (-1, 5), (-1, 3), (-1, 11), (-1, 8), (-1, 6), (-1, 0), (-1, 15))},
     ),
     (
-        "HGGBBGGBHGHBHAAB",
-        {(0, "up"): (4, 8, 10, 14, 7, 13, 15, 3, 11, 12, 0), (0, "down"): (2, 9, 1, 6, 5), (1, "up"): (6, 5, 2, 1, 9), (1, "down"): (0, 10, 8, 12), (2, "up"): (0, 8, 10, 12), (2, "down"): (11, 7, 3, 15, 4)},
-        {0: ((-1, 0), (-1, 10), (-1, 8), (-1, 12), (-1, 11), (-1, 7), (-1, 3), (-1, 15), (-1, 4)), 1: ((1, 4), (-1, 11), (-1, 7), (-1, 3), (1, 14), (-1, 15), (1, 7), (-1, 4), (1, 13), (1, 15), (1, 3), (1, 11)), 2: ((1, 6), (1, 5), (1, 2), (-1, 2), (1, 1), (-1, 9), (1, 9), (-1, 1), (-1, 6), (1, 14), (-1, 5), (1, 13)), 3: ((-1, 2), (-1, 9), (-1, 1), (-1, 6), (-1, 5), (-1, 0), (-1, 10), (-1, 8), (-1, 12))},
+        "HGGBBGGGHBHBHAAB",
+        {(0, "up"): (4, 8, 9, 12, 14, 13, 15, 3, 11, 10, 0), (0, "down"): (2, 7, 1, 6, 5), (1, "up"): (6, 5, 2, 1, 7), (1, "down"): (0, 10, 8, 12), (2, "up"): (0, 8, 10, 12), (2, "down"): (11, 9, 3, 15, 4)},
+        {0: ((-1, 0), (-1, 10), (-1, 8), (-1, 12), (-1, 11), (-1, 9), (-1, 3), (-1, 15), (-1, 4)), 1: ((1, 4), (-1, 11), (-1, 9), (1, 9), (-1, 3), (-1, 15), (1, 14), (-1, 4), (1, 13), (1, 15), (1, 3), (1, 11)), 2: ((1, 6), (1, 5), (1, 2), (-1, 2), (1, 1), (-1, 7), (1, 7), (-1, 1), (-1, 6), (-1, 5), (1, 14), (1, 13)), 3: ((-1, 2), (-1, 7), (-1, 1), (-1, 6), (-1, 5), (-1, 0), (-1, 10), (-1, 8), (-1, 12))},
     ),
 )
 ENDS = {0: [], 1: [("down", "G"), ("up", "H")], 2: [("down", "H"), ("up", "B")], 3: [("up", "H"), ("up", "G"), ("down", "B"), ("up", "A")]}

time: 117 us -> 117 us (level)
  no operation moved by 1% of the time
where the time goes in v7:
time: 117 us; the launch traced here: 115 us
  Pallas kernels  114 us (97%)
    pallas_call x1, Pallas kernels, shards(): pl.pallas_call(functools.partial(steps_kernel, grid_j), out_shape=(pltpu....  108 us
    pallas_call x1, Pallas kernels, shards(): pl.pallas_call(functools.partial(outputs_kernel, grid_j), out_shape=(jax....  5.96 us

profile of v7, /device:TPU:103, one launch (start us, length us, event | category | flops | bytes accessed | tf_op | source)
XLA Modules:
  0.0 114.8 jit_solution(6647754711488180852)
XLA Ops:
  0.6 108.2 %steps.1 = (f32[10,18,128,128]{3,2,1,0:T(8,128)S(1)}, f32[16,128,128]{2,1,0:T(8,128)S(1)}) custom-call(f32[8,16,128,128]{3,2,1,0:T(8,128)} %u0.1, f32[8,16,128,128]{3,2,1,0:T(8,128)} %e0.1, f32[8,16,128,128]{3,2,1,0:T(8,128)} %s0.1), custom_call_target="tpu_custom_call" | custom-call | tf_op jit(solution)/shard_map/steps/pallas_call | solution.py:351
  108.8 6.0 %outputs.1 = (f32[8,16,128,128]{3,2,1,0:T(8,128)}, f32[8,16,128,128]{3,2,1,0:T(8,128)}) custom-call(f32[10,18,128,128]{3,2,1,0:T(8,128)S(1)} %get-tuple-element.4.field, f32[16,128,128]{2,1,0:T(8,128)S(1)} %get-tuple-element.5.below), custom_call_target="tpu_custom_call" | custom-call | tf_op jit(solution)/shard_map/outputs/pallas_call | solution.py:374
